TPU v7x, 32 devices: a whole 2x2x4 slice. The times are simulated.
32 devices in a mesh: gx: 8 (over y, x, core), gy: 4 (over z).
Axes of the slice: x: 2, y: 2, z: 4, core: 2. Of those that a mesh axis runs over, the one named last changes fastest.
Arguments:
- sky_interface_transfers: bfloat16 [4, 384, 1024], P(None, 'gy', 'gx'), may hold values from -6 to 6
- coupling_matrix_enlarged: bfloat16 [384, 1024, 128], P('gy', 'gx'), may hold values from -0.5 to 0.5
- piece_keeper_part: int32 [8, 384, 1], P('gx', 'gy'), may hold values from 0 to 31; in each aligned block of 96 rows (0 to 95, 96 to 191, ..., all dimensions but the last counted through in order) at most 6 rows name the same one
- receiving_part_line: int32 [8, 384], P('gx', 'gy'), may hold values from 0 to 127
- marine_point_switch: int32 [1024, 512], P('gx', 'gy'), may hold values 0 or 1
- potential_heat_deviation: float32 [8, 1024, 512], P(None, 'gx', 'gy'), may hold values from -6 to 6
- free_marine_lift: float32 [1024, 512], P('gx', 'gy'), may hold values from -3 to 3
- depth_averaged_uflow: float32 [1024, 512], P('gx', 'gy'), may hold values from -3 to 3
- depth_averaged_vflow: float32 [1024, 512], P('gx', 'gy'), may hold values from -3 to 3
Outputs:
- atmo_skin_temp_back: float32 [384, 1024], P('gy', 'gx')
- ocean_temp_after_step: float32 [8, 1024, 512], P(None, 'gx', 'gy')
- barotropic: float32 [3, 1024, 512], P(None, 'gx', 'gy')
Inputs may be any that keep to these rules, and one draw needn't show every extreme that they name: `piece_keeper_part`: ocean devices are counted with gx slowest. Among the 96 blocks of one atmosphere device at most 6 have the same owner, and some device has exactly 6 with one owner; every ocean device owns some block.
All inputs are finite; a program needn't handle non-finite values. No bound on the sum of `marine_point_switch` on one device may be relied on, other than what follows from the above.
Results may differ from a plain program's by a relative error of at most 0.0026.
Values may be sent and summed in bfloat16 or wider, within the bound.
A program may use at most 64 MiB of HBM per device.

v0:
```python
import jax
import jax.numpy as jnp
from jax import lax
from jax.sharding import PartitionSpec as P

NB = 96
OX = 128
BAND_NORTH_COUNT = 128
MARINE_STRATA = 8
SUB = 40
DEPTH = 4


HORIZ_MIX = 0.15
VERT_MIX = 0.2
HEAT_GAIN = 0.5
FLOW_DAMP = 0.98
PRESS_GAIN = 0.6
DIVERGE_GAIN = 0.6
CORIOLIS = 0.1
WIND_GAIN = 0.05
FRESH_GAIN = 0.05


def padded(x, sides, width):
    for axis, dim in sides:
        size, length = (lax.axis_size(axis), x.shape[dim])
        up = [(i, (i + 1) % size) for i in range(size)]
        down = [(j, i) for i, j in up]
        last = lax.slice_in_dim(x, length - width, length, axis=dim)
        first = lax.slice_in_dim(x, 0, width, axis=dim)
        before = lax.ppermute(last, axis, up)
        after = lax.ppermute(first, axis, down)
        x = jnp.concatenate([before, x, after], axis=dim)
    return x


def velocity(
    height_rim,
    east_flow_component,
    north_flow_component,
    stress_east,
    stress_north,
    turning,
    liquid_portion,
):
    slope_east = height_rim[2:, 1:-1] - height_rim[:-2, 1:-1]
    slope_north = height_rim[1:-1, 2:] - height_rim[1:-1, :-2]
    zonal_new = (
        FLOW_DAMP * east_flow_component
        - PRESS_GAIN * slope_east
        + turning * north_flow_component
        + WIND_GAIN * stress_east
    ) * liquid_portion
    merid_new = (
        FLOW_DAMP * north_flow_component
        - PRESS_GAIN * slope_north
        - turning * zonal_new
        + WIND_GAIN * stress_north
    ) * liquid_portion
    return (zonal_new, merid_new)


def height(oceanic_top_sheet, zonal_rim, merid_rim, fresh_in, liquid_portion):
    spread = (
        zonal_rim[2:, 1:-1] - zonal_rim[:-2, 1:-1] + (merid_rim[1:-1, 2:] - merid_rim[1:-1, :-2])
    )
    return (oceanic_top_sheet - DIVERGE_GAIN * spread - FRESH_GAIN * fresh_in) * liquid_portion


def integrate_scalar_once(
    heat_deviation, heat_deviation_fringe, liquid_portion_fringe, incoming_enthalpy, liquid_portion
):
    horizontal_diffusion = liquid_portion_fringe[2:, 1:-1] * (
        heat_deviation_fringe[:, 2:, 1:-1] - heat_deviation
    )
    horizontal_diffusion = horizontal_diffusion + liquid_portion_fringe[:-2, 1:-1] * (
        heat_deviation_fringe[:, :-2, 1:-1] - heat_deviation
    )
    horizontal_diffusion = horizontal_diffusion + liquid_portion_fringe[1:-1, 2:] * (
        heat_deviation_fringe[:, 1:-1, 2:] - heat_deviation
    )
    horizontal_diffusion = horizontal_diffusion + liquid_portion_fringe[1:-1, :-2] * (
        heat_deviation_fringe[:, 1:-1, :-2] - heat_deviation
    )
    above_level = jnp.concatenate([heat_deviation[:1], heat_deviation[:-1]], axis=0)
    below_level = jnp.concatenate([heat_deviation[1:], heat_deviation[-1:]], axis=0)
    vertical = above_level - heat_deviation + (below_level - heat_deviation)
    tendency = heat_deviation + HORIZ_MIX * horizontal_diffusion + VERT_MIX * vertical
    tendency = tendency.at[0].add(HEAT_GAIN * incoming_enthalpy)
    return tendency * liquid_portion


def crop(values, margin):
    return values[margin : values.shape[0] - margin, margin : values.shape[1] - margin]


def per_device(
    sky_interface_transfers,
    coupling_matrix_enlarged,
    piece_keeper_part,
    receiving_part_line,
    marine_point_switch,
    potential_heat_deviation,
    free_marine_lift,
    depth_averaged_uflow,
    depth_averaged_vflow,
):
    width_x = lax.axis_size("gx")
    width_y = lax.axis_size("gy")
    worker_groups = width_x * width_y
    greatest_entries = max(2, 2 * NB // worker_groups)
    slot_count = worker_groups * greatest_entries
    partial_value = jnp.einsum(
        "fnc,nco->nfo",
        sky_interface_transfers,
        coupling_matrix_enlarged,
        preferred_element_type=jnp.float32,
    )
    target = piece_keeper_part[0, :, 0]
    hit_table = (target[:, None] == jnp.arange(worker_groups, dtype=jnp.int32)[None, :]).astype(
        jnp.int32
    )
    before = jnp.cumsum(hit_table, axis=0) - hit_table
    slot_index = target * greatest_entries + jnp.sum(before * hit_table, axis=1)
    chosen = slot_index[None, :] == jnp.arange(slot_count, dtype=jnp.int32)[:, None]
    packed = jnp.einsum(
        "sn,nfo->sfo", chosen.astype(jnp.float32), partial_value, precision=lax.Precision.HIGHEST
    )
    rows_sent = jnp.sum(chosen.astype(jnp.int32) * receiving_part_line[0][None, :], axis=1)
    arrived, rows_got = (
        lax.all_to_all(
            packed.reshape(worker_groups, greatest_entries, 4, BAND_NORTH_COUNT),
            ("gx", "gy"),
            split_axis=0,
            concat_axis=0,
            tiled=True,
        ),
        lax.all_to_all(
            rows_sent.reshape(worker_groups, greatest_entries),
            ("gx", "gy"),
            split_axis=0,
            concat_axis=0,
            tiled=True,
        ),
    )
    arrived = arrived.reshape(slot_count, 4, BAND_NORTH_COUNT)
    rows_got = rows_got.reshape(slot_count)
    arrival_place = rows_got[:, None] == jnp.arange(OX, dtype=jnp.int32)[None, :]
    marine_interface_transfers = jnp.einsum(
        "sx,sfo->fxo", arrival_place.astype(jnp.float32), arrived, precision=lax.Precision.HIGHEST
    )
    total_y = width_y * BAND_NORTH_COUNT
    rows_sea = lax.axis_index("gy") * BAND_NORTH_COUNT + jnp.arange(
        BAND_NORTH_COUNT, dtype=jnp.int32
    )
    wall_mask = ((rows_sea > 0) & (rows_sea < total_y - 1)).astype(jnp.float32)
    liquid_portion = marine_point_switch.astype(jnp.float32) * wall_mask[None, :]
    gathered_pieces = jnp.concatenate([potential_heat_deviation, liquid_portion[None]], axis=0)
    with_halo_cells = padded(gathered_pieces, (("gx", 1), ("gy", 2)), 1)
    ocean_temp_after_step = integrate_scalar_once(
        potential_heat_deviation,
        with_halo_cells[:MARINE_STRATA],
        with_halo_cells[MARINE_STRATA],
        marine_interface_transfers[2],
        liquid_portion,
    )
    coupled_skin_warmness = ocean_temp_after_step[0].astype(jnp.bfloat16)
    coupled_skin_warmness_band = jnp.dot(
        arrival_place.astype(jnp.bfloat16),
        coupled_skin_warmness,
        preferred_element_type=jnp.float32,
    ).astype(jnp.bfloat16)
    skin_back = lax.all_to_all(
        coupled_skin_warmness_band.reshape(worker_groups, greatest_entries, BAND_NORTH_COUNT),
        ("gx", "gy"),
        split_axis=0,
        concat_axis=0,
        tiled=True,
    )
    skin_mine = jnp.einsum(
        "sn,so->no",
        chosen.astype(jnp.bfloat16),
        skin_back.reshape(slot_count, BAND_NORTH_COUNT),
        preferred_element_type=jnp.float32,
    ).astype(jnp.bfloat16)
    atmo_skin_temp_back = jnp.einsum(
        "nco,no->nc", coupling_matrix_enlarged, skin_mine, preferred_element_type=jnp.float32
    )
    rim_cells = 2 * DEPTH
    rows_wide = jnp.mod(
        lax.axis_index("gy") * BAND_NORTH_COUNT
        - rim_cells
        + jnp.arange(BAND_NORTH_COUNT + 2 * rim_cells, dtype=jnp.int32),
        total_y,
    )
    turning_row = CORIOLIS * jnp.sin(
        jnp.pi * ((rows_wide.astype(jnp.float32) + 0.5) / total_y - 0.5)
    )
    turning_wide = jnp.broadcast_to(
        turning_row[None, :], (OX + 2 * rim_cells, BAND_NORTH_COUNT + 2 * rim_cells)
    )
    forcing = padded(
        jnp.stack(
            [
                marine_interface_transfers[0],
                marine_interface_transfers[1],
                marine_interface_transfers[3],
                liquid_portion,
            ]
        ),
        (("gx", 1), ("gy", 2)),
        rim_cells,
    )

    def advance_deep(counter, carried):
        state_wide = padded(jnp.stack(carried), (("gx", 1), ("gy", 2)), rim_cells)
        oceanic_top_sheet = state_wide[0]
        east_flow_component = state_wide[1]
        north_flow_component = state_wide[2]
        for section_index in range(DEPTH):
            margin = 2 * section_index + 1
            east_flow_component, north_flow_component = velocity(
                oceanic_top_sheet,
                crop(east_flow_component, 1),
                crop(north_flow_component, 1),
                crop(forcing[0], margin),
                crop(forcing[1], margin),
                crop(turning_wide, margin),
                crop(forcing[3], margin),
            )
            oceanic_top_sheet = height(
                crop(oceanic_top_sheet, 2),
                east_flow_component,
                north_flow_component,
                crop(forcing[2], margin + 1),
                crop(forcing[3], margin + 1),
            )
            east_flow_component = crop(east_flow_component, 1)
            north_flow_component = crop(north_flow_component, 1)
        return (oceanic_top_sheet, east_flow_component, north_flow_component)

    vertical_mean_flow_answer = lax.fori_loop(
        0,
        SUB // DEPTH,
        advance_deep,
        (free_marine_lift, depth_averaged_uflow, depth_averaged_vflow),
    )
    return (atmo_skin_temp_back, ocean_temp_after_step, jnp.stack(vertical_mean_flow_answer))


def solution(mesh):
    in_specs = (
        P(None, "gy", "gx"),
        P("gy", "gx", None),
        P("gx", "gy", None),
        P("gx", "gy"),
        P("gx", "gy"),
        P(None, "gx", "gy"),
        P("gx", "gy"),
        P("gx", "gy"),
        P("gx", "gy"),
    )
    out_specs = (P("gy", "gx"), P(None, "gx", "gy"), P(None, "gx", "gy"))
    return jax.shard_map(
        per_device, mesh=mesh, in_specs=in_specs, out_specs=out_specs, check_vma=False
    )
```

profile of v0, /device:TPU:0, one launch (start us, length us, event | category | flops | bytes accessed | tf_op | source)
XLA Modules:
  0.0 336.5 jit_solution(6353694148475488547)
XLA Ops:
  5.9 2.9 collective-permute-start.5
  12.7 5.6 %all-to-all-start = ((s32[32,1,6]{2,1,0:T(1,128)}), s32[32,1,6]{2,1,0:T(1,128)S(1)}, u32[]{:S(2)}, u32[]{:S(2)}) async-start(s32[32,1,6]{2,1,0:T(1,128)} %bitcast.12), calls=%async_computation | async-start | bytes 32768 | tf_op jit(solution)/shard_map/all_to_all | solution.py:139
  26.4 5.9 %all-to-all-start.1 = ((f32[32,6,4,128]{3,2,1,0:T(4,128)}), f32[32,6,4,128]{3,2,1,0:T(4,128)}, u32[]{:S(2)}, u32[]{:S(2)}) async-start(f32[32,6,4,128]{3,2,1,0:T(4,128)} %bitcast.62), calls=%async_computation.1 | async-start | bytes 786432 | tf_op jit(solution)/shard_map/all_to_all | solution.py:132
  47.1 3.9 %fusion.62 = f32[8,128,128]{2,1,0:T(8,128)} fusion(f32[8,128,128]{2,1,0:T(8,128)} %param.18, f32[9,130,1]{2,1,0:T(8,128)} %copy.17, f32[9,1,128]{2,1,0:T(1,128)S(1)} %collective-permute-done.5, f32[9,1,128]{2,1,0:T(1,128)S(1)} %collective-permute-done.4, f32[1,128,128]{2,1,0:T(8,128)S(1)} %fusion.117, f32[9,130,1]{2,1,0:T(8,128)} %copy.18, ...), kind=kLoop, calls=%fused_computation.116 | loop fusion | flops 4194304 | bytes 2443408 | tf_op jit(solution)/shard_map/add | solution.py:89
  54.0 2.6 collective-permute-start.9
  59.5 3.2 collective-permute-start.11
  63.6 3.2 all-to-all-start.2
  66.9 4.1 %collective-permute-done.10 = f32[4,144,8]{2,1,0:T(8,128)} collective-permute-done((f32[4,144,8]{2,1,0:T(8,128)}, f32[4,144,8]{2,1,0:T(8,128)}, u32[]{:S(2)}, u32[]{:S(2)}) %collective-permute-start.10) | collective-permute-done | bytes 18464 | tf_op jit(solution)/shard_map/ppermute | solution.py:32
  71.0 4.7 %collective-permute-done.11 = f32[4,144,8]{2,1,0:T(8,128)} collective-permute-done((f32[4,144,8]{2,1,0:T(8,128)}, f32[4,144,8]{2,1,0:T(8,128)}, u32[]{:S(2)}, u32[]{:S(2)}) %collective-permute-start.11) | collective-permute-done | bytes 18464 | tf_op jit(solution)/shard_map/ppermute | solution.py:33
  79.1 252.3 %while.15 = (s32[]{:T(128)}, f32[128,128]{1,0:T(8,128)S(1)}, f32[128,128]{1,0:T(8,128)}, f32[128,128]{1,0:T(8,128)}, f32[144,144]{1,0:T(8,128)}, /*index=5*/f32[4,144,144]{2,1,0:T(8,128)}, s32[]{:T(128)}) while((s32[]{:T(128)}, f32[128,128]{1,0:T(8,128)S(1)}, f32[128,128]{1,0:T(8,128)}, f32[128,128]{1,0:T(8,128)}, f32[144,144]{1,0:T(8,128)}, ...), condition=%wide.region_4.5_spmd, body=%wide.region_3.4_spmd.sunk | while | flops 2515106 | bytes 9700417 | solution.py:243
  83.1 2.6 collective-permute-done.1
  91.5 4.5 %collective-permute-done.2 = f32[3,144,8]{2,1,0:T(8,128)} collective-permute-done((f32[3,144,8]{2,1,0:T(8,128)}, f32[3,144,8]{2,1,0:T(8,128)}, u32[]{:S(2)}, u32[]{:S(2)}) %collective-permute-start.2) | collective-permute-done | bytes 13856 | tf_op jit(solution)/shard_map/while/body/eval_jaxpr/ppermute | solution.py:33
  96.0 2.7 collective-permute-done.3
  105.2 2.6 collective-permute-start
  109.3 2.6 collective-permute-done.1
  117.5 4.2 %collective-permute-done.2 = f32[3,144,8]{2,1,0:T(8,128)} collective-permute-done((f32[3,144,8]{2,1,0:T(8,128)}, f32[3,144,8]{2,1,0:T(8,128)}, u32[]{:S(2)}, u32[]{:S(2)}) %collective-permute-start.2) | collective-permute-done | bytes 13856 | tf_op jit(solution)/shard_map/while/body/eval_jaxpr/ppermute | solution.py:33
  134.5 2.6 collective-permute-done.1
  142.8 3.9 %collective-permute-done.2 = f32[3,144,8]{2,1,0:T(8,128)} collective-permute-done((f32[3,144,8]{2,1,0:T(8,128)}, f32[3,144,8]{2,1,0:T(8,128)}, u32[]{:S(2)}, u32[]{:S(2)}) %collective-permute-start.2) | collective-permute-done | bytes 13856 | tf_op jit(solution)/shard_map/while/body/eval_jaxpr/ppermute | solution.py:33
  159.4 2.6 collective-permute-done.1
  167.7 4.4 %collective-permute-done.2 = f32[3,144,8]{2,1,0:T(8,128)} collective-permute-done((f32[3,144,8]{2,1,0:T(8,128)}, f32[3,144,8]{2,1,0:T(8,128)}, u32[]{:S(2)}, u32[]{:S(2)}) %collective-permute-start.2) | collective-permute-done | bytes 13856 | tf_op jit(solution)/shard_map/while/body/eval_jaxpr/ppermute | solution.py:33
  183.5 2.6 collective-permute-done.1
  191.8 4.7 %collective-permute-done.2 = f32[3,144,8]{2,1,0:T(8,128)} collective-permute-done((f32[3,144,8]{2,1,0:T(8,128)}, f32[3,144,8]{2,1,0:T(8,128)}, u32[]{:S(2)}, u32[]{:S(2)}) %collective-permute-start.2) | collective-permute-done | bytes 13856 | tf_op jit(solution)/shard_map/while/body/eval_jaxpr/ppermute | solution.py:33
  196.5 3.0 collective-permute-done.3
  209.9 2.6 collective-permute-done.1
  218.2 4.4 %collective-permute-done.2 = f32[3,144,8]{2,1,0:T(8,128)} collective-permute-done((f32[3,144,8]{2,1,0:T(8,128)}, f32[3,144,8]{2,1,0:T(8,128)}, u32[]{:S(2)}, u32[]{:S(2)}) %collective-permute-start.2) | collective-permute-done | bytes 13856 | tf_op jit(solution)/shard_map/while/body/eval_jaxpr/ppermute | solution.py:33
  234.7 2.6 collective-permute-done.1
  242.9 4.7 %collective-permute-done.2 = f32[3,144,8]{2,1,0:T(8,128)} collective-permute-done((f32[3,144,8]{2,1,0:T(8,128)}, f32[3,144,8]{2,1,0:T(8,128)}, u32[]{:S(2)}, u32[]{:S(2)}) %collective-permute-start.2) | collective-permute-done | bytes 13856 | tf_op jit(solution)/shard_map/while/body/eval_jaxpr/ppermute | solution.py:33
  247.6 2.7 collective-permute-done.3
  268.0 4.7 %collective-permute-done.2 = f32[3,144,8]{2,1,0:T(8,128)} collective-permute-done((f32[3,144,8]{2,1,0:T(8,128)}, f32[3,144,8]{2,1,0:T(8,128)}, u32[]{:S(2)}, u32[]{:S(2)}) %collective-permute-start.2) | collective-permute-done | bytes 13856 | tf_op jit(solution)/shard_map/while/body/eval_jaxpr/ppermute | solution.py:33
  272.7 3.0 collective-permute-done.3
  294.1 4.0 %collective-permute-done.2 = f32[3,144,8]{2,1,0:T(8,128)} collective-permute-done((f32[3,144,8]{2,1,0:T(8,128)}, f32[3,144,8]{2,1,0:T(8,128)}, u32[]{:S(2)}, u32[]{:S(2)}) %collective-permute-start.2) | collective-permute-done | bytes 13856 | tf_op jit(solution)/shard_map/while/body/eval_jaxpr/ppermute | solution.py:33
  318.5 4.7 %collective-permute-done.2 = f32[3,144,8]{2,1,0:T(8,128)} collective-permute-done((f32[3,144,8]{2,1,0:T(8,128)}, f32[3,144,8]{2,1,0:T(8,128)}, u32[]{:S(2)}, u32[]{:S(2)}) %collective-permute-start.2) | collective-permute-done | bytes 13856 | tf_op jit(solution)/shard_map/while/body/eval_jaxpr/ppermute | solution.py:33
  (340 shorter events, 222.0 us)
Async XLA Ops:
  5.4 19.1 %collective-permute-start.4 = (f32[9,1,128]{2,1,0:T(1,128)S(1)}, f32[9,1,128]{2,1,0:T(1,128)S(1)}, u32[]{:S(2)}, u32[]{:S(2)}) collective-permute-start(f32[9,1,128]{2,1,0:T(1,128)S(1)} %get-tuple-element.88), channel_id=1, source_target_pairs={{0,4},{4,8},{8,12},{12,16},{16,20},{20,24},{24,28},{28,0},{1,5},{5... | collective-permute-start | bytes 13832 | tf_op jit(solution)/shard_map/ppermute | solution.py:32
  5.9 18.5 %collective-permute-start.5 = (f32[9,1,128]{2,1,0:T(1,128)S(1)}, f32[9,1,128]{2,1,0:T(1,128)S(1)}, u32[]{:S(2)}, u32[]{:S(2)}) collective-permute-start(f32[9,1,128]{2,1,0:T(1,128)S(1)} %get-tuple-element.89), channel_id=1, source_target_pairs={{4,0},{8,4},{12,8},{16,12},{20,16},{24,20},{28,24},{0,28},{5,1},{9... | collective-permute-start | bytes 13832 | tf_op jit(solution)/shard_map/ppermute | solution.py:33
  12.7 13.7 %all-to-all-start = ((s32[32,1,6]{2,1,0:T(1,128)}), s32[32,1,6]{2,1,0:T(1,128)S(1)}, u32[]{:S(2)}, u32[]{:S(2)}) async-start(s32[32,1,6]{2,1,0:T(1,128)} %bitcast.12), calls=%async_computation | async-start | bytes 32768 | tf_op jit(solution)/shard_map/all_to_all | solution.py:139
  26.4 24.6 %all-to-all-start.1 = ((f32[32,6,4,128]{3,2,1,0:T(4,128)}), f32[32,6,4,128]{3,2,1,0:T(4,128)}, u32[]{:S(2)}, u32[]{:S(2)}) async-start(f32[32,6,4,128]{3,2,1,0:T(4,128)} %bitcast.62), calls=%async_computation.1 | async-start | bytes 786432 | tf_op jit(solution)/shard_map/all_to_all | solution.py:132
  36.4 7.3 %collective-permute-start.6 = (f32[9,130,1]{1,2,0:T(1,128)S(1)}, f32[9,130,1]{1,2,0:T(1,128)S(1)}, u32[]{:S(2)}, u32[]{:S(2)}) collective-permute-start(f32[9,130,1]{1,2,0:T(1,128)S(1)} %copy.15), channel_id=1, source_target_pairs={{0,1},{1,2},{2,3},{3,0},{4,5},{5,6},{6,7},{7,4},{8,9},{9,10},{10,1... | collective-permute-start | bytes 14048 | tf_op jit(solution)/shard_map/ppermute | solution.py:32
  39.5 5.2 %collective-permute-start.7 = (f32[9,130,1]{1,2,0:T(1,128)S(1)}, f32[9,130,1]{1,2,0:T(1,128)S(1)}, u32[]{:S(2)}, u32[]{:S(2)}) collective-permute-start(f32[9,130,1]{1,2,0:T(1,128)S(1)} %copy.16), channel_id=1, source_target_pairs={{1,0},{2,1},{3,2},{0,3},{5,4},{6,5},{7,6},{4,7},{9,8},{10,9},{11,1... | collective-permute-start | bytes 14048 | tf_op jit(solution)/shard_map/ppermute | solution.py:33
  54.0 4.1 %collective-permute-start.8 = (f32[4,8,128]{2,1,0:T(8,128)S(1)}, f32[4,8,128]{2,1,0:T(8,128)S(1)}, u32[]{:S(2)}, u32[]{:S(2)}) collective-permute-start(f32[4,8,128]{2,1,0:T(8,128)S(1)} %get-tuple-element.96), channel_id=1, source_target_pairs={{0,4},{4,8},{8,12},{12,16},{16,20},{20,24},{24,28},{28,0},{1,5},{5... | collective-permute-start | bytes 49160 | tf_op jit(solution)/shard_map/ppermute | solution.py:32
  54.0 4.1 %collective-permute-start.9 = (f32[4,8,128]{2,1,0:T(8,128)S(1)}, f32[4,8,128]{2,1,0:T(8,128)S(1)}, u32[]{:S(2)}, u32[]{:S(2)}) collective-permute-start(f32[4,8,128]{2,1,0:T(8,128)S(1)} %get-tuple-element.97), channel_id=1, source_target_pairs={{4,0},{8,4},{12,8},{16,12},{20,16},{24,20},{28,24},{0,28},{5,1},{9... | collective-permute-start | bytes 49160 | tf_op jit(solution)/shard_map/ppermute | solution.py:33
  59.0 12.0 %collective-permute-start.10 = (f32[4,144,8]{2,1,0:T(8,128)}, f32[4,144,8]{2,1,0:T(8,128)}, u32[]{:S(2)}, u32[]{:S(2)}) collective-permute-start(f32[4,144,8]{2,1,0:T(8,128)} %get-tuple-element.94), channel_id=1, source_target_pairs={{0,1},{1,2},{2,3},{3,0},{4,5},{5,6},{6,7},{7,4},{8,9},{9,10},{10,1... | collective-permute-start | bytes 55304 | tf_op jit(solution)/shard_map/ppermute | solution.py:32
  59.5 16.1 %collective-permute-start.11 = (f32[4,144,8]{2,1,0:T(8,128)}, f32[4,144,8]{2,1,0:T(8,128)}, u32[]{:S(2)}, u32[]{:S(2)}) collective-permute-start(f32[4,144,8]{2,1,0:T(8,128)} %get-tuple-element.95), channel_id=1, source_target_pairs={{1,0},{2,1},{3,2},{0,3},{5,4},{6,5},{7,6},{4,7},{9,8},{10,9},{11,1... | collective-permute-start | bytes 55304 | tf_op jit(solution)/shard_map/ppermute | solution.py:33
  63.6 269.4 %all-to-all-start.2 = ((bf16[32,6,128]{2,1,0:T(8,128)(2,1)}), bf16[32,6,128]{2,1,0:T(8,128)(2,1)}, u32[]{:S(2)}, u32[]{:S(2)}) async-start(bf16[32,6,128]{2,1,0:T(8,128)(2,1)} %reshape.102), calls=%async_computation.2 | async-start | bytes 131072 | tf_op jit(solution)/shard_map/all_to_all | solution.py:174
  87.4 8.6 %collective-permute-start.2 = (f32[3,144,8]{2,1,0:T(8,128)}, f32[3,144,8]{2,1,0:T(8,128)}, u32[]{:S(2)}, u32[]{:S(2)}) collective-permute-start(f32[3,144,8]{2,1,0:T(8,128)} %get-tuple-element.168), channel_id=1, source_target_pairs={{1,0},{2,1},{3,2},{0,3},{5,4},{6,5},{7,6},{4,7},{9,8},{10,9},{11,1... | collective-permute-start | bytes 41480 | tf_op jit(solution)/shard_map/while/body/eval_jaxpr/ppermute | solution.py:33
  89.6 9.1 %collective-permute-start.3 = (f32[3,144,8]{2,1,0:T(8,128)}, f32[3,144,8]{2,1,0:T(8,128)}, u32[]{:S(2)}, u32[]{:S(2)}) collective-permute-start(f32[3,144,8]{2,1,0:T(8,128)} %get-tuple-element.169), channel_id=1, source_target_pairs={{0,1},{1,2},{2,3},{3,0},{4,5},{5,6},{6,7},{7,4},{8,9},{9,10},{10,1... | collective-permute-start | bytes 41480 | tf_op jit(solution)/shard_map/while/body/eval_jaxpr/ppermute | solution.py:32
  105.2 4.0 %collective-permute-start = (f32[3,8,128]{2,1,0:T(8,128)S(1)}, f32[3,8,128]{2,1,0:T(8,128)S(1)}, u32[]{:S(2)}, u32[]{:S(2)}) collective-permute-start(f32[3,8,128]{2,1,0:T(8,128)S(1)} %get-tuple-element.166), channel_id=1, source_target_pairs={{4,0},{8,4},{12,8},{16,12},{20,16},{24,20},{28,24},{0,28},{5,1},{9... | collective-permute-start | bytes 36872 | tf_op jit(solution)/shard_map/while/body/eval_jaxpr/ppermute | solution.py:33
  113.6 8.1 %collective-permute-start.2 = (f32[3,144,8]{2,1,0:T(8,128)}, f32[3,144,8]{2,1,0:T(8,128)}, u32[]{:S(2)}, u32[]{:S(2)}) collective-permute-start(f32[3,144,8]{2,1,0:T(8,128)} %get-tuple-element.168), channel_id=1, source_target_pairs={{1,0},{2,1},{3,2},{0,3},{5,4},{6,5},{7,6},{4,7},{9,8},{10,9},{11,1... | collective-permute-start | bytes 41480 | tf_op jit(solution)/shard_map/while/body/eval_jaxpr/ppermute | solution.py:33
  115.1 9.0 %collective-permute-start.3 = (f32[3,144,8]{2,1,0:T(8,128)}, f32[3,144,8]{2,1,0:T(8,128)}, u32[]{:S(2)}, u32[]{:S(2)}) collective-permute-start(f32[3,144,8]{2,1,0:T(8,128)} %get-tuple-element.169), channel_id=1, source_target_pairs={{0,1},{1,2},{2,3},{3,0},{4,5},{5,6},{6,7},{7,4},{8,9},{9,10},{10,1... | collective-permute-start | bytes 41480 | tf_op jit(solution)/shard_map/while/body/eval_jaxpr/ppermute | solution.py:32
  138.9 7.8 %collective-permute-start.2 = (f32[3,144,8]{2,1,0:T(8,128)}, f32[3,144,8]{2,1,0:T(8,128)}, u32[]{:S(2)}, u32[]{:S(2)}) collective-permute-start(f32[3,144,8]{2,1,0:T(8,128)} %get-tuple-element.168), channel_id=1, source_target_pairs={{1,0},{2,1},{3,2},{0,3},{5,4},{6,5},{7,6},{4,7},{9,8},{10,9},{11,1... | collective-permute-start | bytes 41480 | tf_op jit(solution)/shard_map/while/body/eval_jaxpr/ppermute | solution.py:33
  140.3 8.7 %collective-permute-start.3 = (f32[3,144,8]{2,1,0:T(8,128)}, f32[3,144,8]{2,1,0:T(8,128)}, u32[]{:S(2)}, u32[]{:S(2)}) collective-permute-start(f32[3,144,8]{2,1,0:T(8,128)} %get-tuple-element.169), channel_id=1, source_target_pairs={{0,1},{1,2},{2,3},{3,0},{4,5},{5,6},{6,7},{7,4},{8,9},{9,10},{10,1... | collective-permute-start | bytes 41480 | tf_op jit(solution)/shard_map/while/body/eval_jaxpr/ppermute | solution.py:32
  163.7 8.3 %collective-permute-start.2 = (f32[3,144,8]{2,1,0:T(8,128)}, f32[3,144,8]{2,1,0:T(8,128)}, u32[]{:S(2)}, u32[]{:S(2)}) collective-permute-start(f32[3,144,8]{2,1,0:T(8,128)} %get-tuple-element.168), channel_id=1, source_target_pairs={{1,0},{2,1},{3,2},{0,3},{5,4},{6,5},{7,6},{4,7},{9,8},{10,9},{11,1... | collective-permute-start | bytes 41480 | tf_op jit(solution)/shard_map/while/body/eval_jaxpr/ppermute | solution.py:33
  165.2 9.3 %collective-permute-start.3 = (f32[3,144,8]{2,1,0:T(8,128)}, f32[3,144,8]{2,1,0:T(8,128)}, u32[]{:S(2)}, u32[]{:S(2)}) collective-permute-start(f32[3,144,8]{2,1,0:T(8,128)} %get-tuple-element.169), channel_id=1, source_target_pairs={{0,1},{1,2},{2,3},{3,0},{4,5},{5,6},{6,7},{7,4},{8,9},{9,10},{10,1... | collective-permute-start | bytes 41480 | tf_op jit(solution)/shard_map/while/body/eval_jaxpr/ppermute | solution.py:32
  187.9 8.6 %collective-permute-start.2 = (f32[3,144,8]{2,1,0:T(8,128)}, f32[3,144,8]{2,1,0:T(8,128)}, u32[]{:S(2)}, u32[]{:S(2)}) collective-permute-start(f32[3,144,8]{2,1,0:T(8,128)} %get-tuple-element.168), channel_id=1, source_target_pairs={{1,0},{2,1},{3,2},{0,3},{5,4},{6,5},{7,6},{4,7},{9,8},{10,9},{11,1... | collective-permute-start | bytes 41480 | tf_op jit(solution)/shard_map/while/body/eval_jaxpr/ppermute | solution.py:33
  189.3 10.2 %collective-permute-start.3 = (f32[3,144,8]{2,1,0:T(8,128)}, f32[3,144,8]{2,1,0:T(8,128)}, u32[]{:S(2)}, u32[]{:S(2)}) collective-permute-start(f32[3,144,8]{2,1,0:T(8,128)} %get-tuple-element.169), channel_id=1, source_target_pairs={{0,1},{1,2},{2,3},{3,0},{4,5},{5,6},{6,7},{7,4},{8,9},{9,10},{10,1... | collective-permute-start | bytes 41480 | tf_op jit(solution)/shard_map/while/body/eval_jaxpr/ppermute | solution.py:32
  214.2 8.3 %collective-permute-start.2 = (f32[3,144,8]{2,1,0:T(8,128)}, f32[3,144,8]{2,1,0:T(8,128)}, u32[]{:S(2)}, u32[]{:S(2)}) collective-permute-start(f32[3,144,8]{2,1,0:T(8,128)} %get-tuple-element.168), channel_id=1, source_target_pairs={{1,0},{2,1},{3,2},{0,3},{5,4},{6,5},{7,6},{4,7},{9,8},{10,9},{11,1... | collective-permute-start | bytes 41480 | tf_op jit(solution)/shard_map/while/body/eval_jaxpr/ppermute | solution.py:33
  215.8 9.1 %collective-permute-start.3 = (f32[3,144,8]{2,1,0:T(8,128)}, f32[3,144,8]{2,1,0:T(8,128)}, u32[]{:S(2)}, u32[]{:S(2)}) collective-permute-start(f32[3,144,8]{2,1,0:T(8,128)} %get-tuple-element.169), channel_id=1, source_target_pairs={{0,1},{1,2},{2,3},{3,0},{4,5},{5,6},{6,7},{7,4},{8,9},{9,10},{10,1... | collective-permute-start | bytes 41480 | tf_op jit(solution)/shard_map/while/body/eval_jaxpr/ppermute | solution.py:32
  239.0 8.6 %collective-permute-start.2 = (f32[3,144,8]{2,1,0:T(8,128)}, f32[3,144,8]{2,1,0:T(8,128)}, u32[]{:S(2)}, u32[]{:S(2)}) collective-permute-start(f32[3,144,8]{2,1,0:T(8,128)} %get-tuple-element.168), channel_id=1, source_target_pairs={{1,0},{2,1},{3,2},{0,3},{5,4},{6,5},{7,6},{4,7},{9,8},{10,9},{11,1... | collective-permute-start | bytes 41480 | tf_op jit(solution)/shard_map/while/body/eval_jaxpr/ppermute | solution.py:33
  240.5 9.8 %collective-permute-start.3 = (f32[3,144,8]{2,1,0:T(8,128)}, f32[3,144,8]{2,1,0:T(8,128)}, u32[]{:S(2)}, u32[]{:S(2)}) collective-permute-start(f32[3,144,8]{2,1,0:T(8,128)} %get-tuple-element.169), channel_id=1, source_target_pairs={{0,1},{1,2},{2,3},{3,0},{4,5},{5,6},{6,7},{7,4},{8,9},{9,10},{10,1... | collective-permute-start | bytes 41480 | tf_op jit(solution)/shard_map/while/body/eval_jaxpr/ppermute | solution.py:32
  264.0 8.6 %collective-permute-start.2 = (f32[3,144,8]{2,1,0:T(8,128)}, f32[3,144,8]{2,1,0:T(8,128)}, u32[]{:S(2)}, u32[]{:S(2)}) collective-permute-start(f32[3,144,8]{2,1,0:T(8,128)} %get-tuple-element.168), channel_id=1, source_target_pairs={{1,0},{2,1},{3,2},{0,3},{5,4},{6,5},{7,6},{4,7},{9,8},{10,9},{11,1... | collective-permute-start | bytes 41480 | tf_op jit(solution)/shard_map/while/body/eval_jaxpr/ppermute | solution.py:33
  265.7 9.9 %collective-permute-start.3 = (f32[3,144,8]{2,1,0:T(8,128)}, f32[3,144,8]{2,1,0:T(8,128)}, u32[]{:S(2)}, u32[]{:S(2)}) collective-permute-start(f32[3,144,8]{2,1,0:T(8,128)} %get-tuple-element.169), channel_id=1, source_target_pairs={{0,1},{1,2},{2,3},{3,0},{4,5},{5,6},{6,7},{7,4},{8,9},{9,10},{10,1... | collective-permute-start | bytes 41480 | tf_op jit(solution)/shard_map/while/body/eval_jaxpr/ppermute | solution.py:32
  290.2 7.9 %collective-permute-start.2 = (f32[3,144,8]{2,1,0:T(8,128)}, f32[3,144,8]{2,1,0:T(8,128)}, u32[]{:S(2)}, u32[]{:S(2)}) collective-permute-start(f32[3,144,8]{2,1,0:T(8,128)} %get-tuple-element.168), channel_id=1, source_target_pairs={{1,0},{2,1},{3,2},{0,3},{5,4},{6,5},{7,6},{4,7},{9,8},{10,9},{11,1... | collective-permute-start | bytes 41480 | tf_op jit(solution)/shard_map/while/body/eval_jaxpr/ppermute | solution.py:33
  291.7 8.8 %collective-permute-start.3 = (f32[3,144,8]{2,1,0:T(8,128)}, f32[3,144,8]{2,1,0:T(8,128)}, u32[]{:S(2)}, u32[]{:S(2)}) collective-permute-start(f32[3,144,8]{2,1,0:T(8,128)} %get-tuple-element.169), channel_id=1, source_target_pairs={{0,1},{1,2},{2,3},{3,0},{4,5},{5,6},{6,7},{7,4},{8,9},{9,10},{10,1... | collective-permute-start | bytes 41480 | tf_op jit(solution)/shard_map/while/body/eval_jaxpr/ppermute | solution.py:32
  314.6 8.6 %collective-permute-start.2 = (f32[3,144,8]{2,1,0:T(8,128)}, f32[3,144,8]{2,1,0:T(8,128)}, u32[]{:S(2)}, u32[]{:S(2)}) collective-permute-start(f32[3,144,8]{2,1,0:T(8,128)} %get-tuple-element.168), channel_id=1, source_target_pairs={{1,0},{2,1},{3,2},{0,3},{5,4},{6,5},{7,6},{4,7},{9,8},{10,9},{11,1... | collective-permute-start | bytes 41480 | tf_op jit(solution)/shard_map/while/body/eval_jaxpr/ppermute | solution.py:33
  316.1 9.6 %collective-permute-start.3 = (f32[3,144,8]{2,1,0:T(8,128)}, f32[3,144,8]{2,1,0:T(8,128)}, u32[]{:S(2)}, u32[]{:S(2)}) collective-permute-start(f32[3,144,8]{2,1,0:T(8,128)} %get-tuple-element.169), channel_id=1, source_target_pairs={{0,1},{1,2},{2,3},{3,0},{4,5},{5,6},{6,7},{7,4},{8,9},{9,10},{10,1... | collective-permute-start | bytes 41480 | tf_op jit(solution)/shard_map/while/body/eval_jaxpr/ppermute | solution.py:32
  (61 other events, 746.0 us)
where the time goes:
time: 339 us; the launch traced here: 336 us
  waiting for transfers between devices  119 us (35%)
  other arithmetic  92.9 us (27%)
  starting transfers between devices  69.8 us (21%)
  local copies, waits for them, and re-layouts  47.6 us (14%)
  matrix products  5.43 us (2%)
    ppermute x24, waiting for transfers between devices, padded(): after = lax.ppermute(first, axis, down)  62.8 us
    ppermute x24, waiting for transfers between devices, padded(): before = lax.ppermute(last, axis, up)  56.2 us
    ppermute x24, starting transfers between devices, padded(): after = lax.ppermute(first, axis, down)  47.3 us
    concatenate x23, other arithmetic, padded(): x = jnp.concatenate([before, x, after], axis=dim)  26.4 us
    mul x40, other arithmetic, velocity(): (FLOW_DAMP * north_flow_component - PRESS_GAIN * slope_north - turning *...  26.2 us
    squeeze x10, local copies, waits for them, and re-layouts, advance_deep(): forcing[0]  18.9 us
    slice x12, local copies, waits for them, and re-layouts, padded(): last = lax.slice_in_dim(x, length - width, length, axis=dim)  10.5 us
    mul x30, other arithmetic, height(): (oceanic_top_sheet - DIVERGE_GAIN * spread - FRESH_GAIN * fresh_in) * liq...  8.83 us
  transfers between devices with their start and end apart: 51, of which 43 were waited for; matrix products, arithmetic and copies ran while one was open for 40% of the time, Pallas kernels for 0%

commit v1 on v0

--- a/solution.py
+++ b/solution.py
@@ -1,6 +1,8 @@
 import jax
 import jax.numpy as jnp
 from jax import lax
+from jax.experimental import pallas as pl
+from jax.experimental.pallas import tpu as pltpu
 from jax.sharding import PartitionSpec as P
 
 NB = 96
@@ -8,7 +10,6 @@
 BAND_NORTH_COUNT = 128
 MARINE_STRATA = 8
 SUB = 40
-DEPTH = 4
 
 
 HORIZ_MIX = 0.15
@@ -35,37 +36,236 @@
     return x
 
 
-def velocity(
-    height_rim,
-    east_flow_component,
-    north_flow_component,
-    stress_east,
-    stress_north,
-    turning,
-    liquid_portion,
+MESH = pl.DeviceIdType.MESH
+HALF = BAND_NORTH_COUNT // 2
+WIDE = OX + 2 * HALF
+PACK = HALF // 2
+SPAN = SUB // 2
+CHUNK = 16
+
+
+def low_lanes(rows):
+    return lax.broadcasted_iota(jnp.int32, (rows, BAND_NORTH_COUNT), 1) < HALF
+
+
+def pack_half(values):
+    low = low_lanes(PACK)
+    first, second = values[:PACK], pltpu.roll(values[PACK:], HALF, 1)
+    return (
+        jnp.where(low, first, second).astype(jnp.bfloat16),
+        jnp.where(low, second, first).astype(jnp.bfloat16),
+    )
+
+
+def unpack_half(low_quadrant, high_quadrant):
+    low = low_lanes(PACK)
+    lo = low_quadrant.astype(jnp.float32)
+    hi = high_quadrant.astype(jnp.float32)
+    return jnp.where(low, lo, hi), pltpu.roll(jnp.where(low, hi, lo), HALF, 1)
+
+
+def neighbours():
+    nx, ny = lax.axis_size("gx"), lax.axis_size("gy")
+    x, y = lax.axis_index("gx"), lax.axis_index("gy")
+    up, down = lax.rem(x + 1, nx), lax.rem(x + nx - 1, nx)
+    right, left = lax.rem(y + 1, ny), lax.rem(y + ny - 1, ny)
+    return x, y, up, down, right, left
+
+
+def greet():
+    x, y, up, down, right, left = neighbours()
+    barrier = pltpu.get_barrier_semaphore()
+    for place in (
+        (up, y),
+        (down, y),
+        (x, right),
+        (x, left),
+        (up, right),
+        (up, left),
+        (down, right),
+        (down, left),
+    ):
+        pl.semaphore_signal(barrier, inc=1, device_id=place, device_id_type=MESH)
+    pl.semaphore_wait(barrier, 8)
+
+
+def margin_copies(quads, edge, side, send_sem, recv_sem):
+    x, y, up, down, right, left = neighbours()
+    plan = (
+        (quads.at[1], edge.at[0], (up, y)),
+        (quads.at[0], edge.at[1], (down, y)),
+        (quads.at[0, 1], side.at[1, 1], (x, right)),
+        (quads.at[1, 1], side.at[2, 1], (x, right)),
+        (quads.at[0, 0], side.at[1, 0], (x, left)),
+        (quads.at[1, 0], side.at[2, 0], (x, left)),
+        (quads.at[1, 1], side.at[0, 1], (up, right)),
+        (quads.at[1, 0], side.at[0, 0], (up, left)),
+        (quads.at[0, 1], side.at[3, 1], (down, right)),
+        (quads.at[0, 0], side.at[3, 0], (down, left)),
+    )
+    return [
+        pltpu.make_async_remote_copy(
+            src_ref=src,
+            dst_ref=dst,
+            send_sem=send_sem.at[k],
+            recv_sem=recv_sem.at[k],
+            device_id=place,
+            device_id_type=MESH,
+        )
+        for k, (src, dst, place) in enumerate(plan)
+    ]
+
+
+def fill_quads(quads, field, values):
+    for part in range(2):
+        lo, hi = pack_half(values[part * HALF : (part + 1) * HALF])
+        quads[part, 0, field] = lo
+        quads[part, 1, field] = hi
+
+
+def spread_margin(edge, side, field, wide):
+    for row_block in range(4):
+        start = row_block * HALF
+        if row_block in (0, 3):
+            at = 0 if row_block == 0 else 1
+            one, two = unpack_half(edge[at, 0, field], edge[at, 1, field])
+            wide[0, start : start + PACK] = one
+            wide[0, start + PACK : start + HALF] = two
+        one, two = unpack_half(side[row_block, 0, field], side[row_block, 1, field])
+        wide[1, start : start + PACK] = one
+        wide[1, start + PACK : start + HALF] = two
+
+
+def lat_difference(own, far):
+    lane = lax.broadcasted_iota(jnp.int32, own.shape, 1)
+    last, first = lane == BAND_NORTH_COUNT - 1, lane == 0
+    own_up = pltpu.roll(own, BAND_NORTH_COUNT - 1, 1)
+    far_up = pltpu.roll(far, BAND_NORTH_COUNT - 1, 1)
+    own_down = pltpu.roll(own, 1, 1)
+    far_down = pltpu.roll(far, 1, 1)
+    return (
+        jnp.where(last, far_up, own_up) - jnp.where(first, far_down, own_down),
+        jnp.where(last, own_up, far_up) - jnp.where(first, own_down, far_down),
+    )
+
+
+def substep(reach, h, u, v, east, north, fresh, wet, turning):
+    low, high = HALF - reach, HALF + OX + reach
+    turn = [
+        jnp.broadcast_to(turning[tile : tile + 1, :], (CHUNK, BAND_NORTH_COUNT))
+        for tile in range(2)
+    ]
+    for start in range(low, high, CHUNK):
+        rows = slice(start, start + CHUNK)
+        slope_north = lat_difference(h[0, rows], h[1, rows])
+        for tile in range(2):
+            slope_east = (
+                h[tile, start + 1 : start + CHUNK + 1] - h[tile, start - 1 : start + CHUNK - 1]
+            )
+            old_u, old_v, mask = u[tile, rows], v[tile, rows], wet[tile, rows]
+            new_u = (
+                FLOW_DAMP * old_u - PRESS_GAIN * slope_east + turn[tile] * old_v + east[tile, rows]
+            ) * mask
+            u[tile, rows] = new_u
+            v[tile, rows] = (
+                FLOW_DAMP * old_v
+                - PRESS_GAIN * slope_north[tile]
+                - turn[tile] * new_u
+                + north[tile, rows]
+            ) * mask
+    for start in range(low, high, CHUNK):
+        rows = slice(start, start + CHUNK)
+        spread_north = lat_difference(v[0, rows], v[1, rows])
+        for tile in range(2):
+            spread_east = (
+                u[tile, start + 1 : start + CHUNK + 1] - u[tile, start - 1 : start + CHUNK - 1]
+            )
+            h[tile, rows] = (
+                h[tile, rows]
+                - DIVERGE_GAIN * (spread_east + spread_north[tile])
+                - fresh[tile, rows]
+            ) * wet[tile, rows]
+
+
+def run_span(h, u, v, east, north, fresh, wet, turning):
+    done = 0
+    while done < SPAN:
+        need = 2 * (SPAN - done) - 1
+        reach = -(-need // 8) * 8
+        steps = min(SPAN - done, 4)
+
+        def one(_, carry, reach=reach):
+            substep(reach, h, u, v, east, north, fresh, wet, turning)
+            return carry
+
+        lax.fori_loop(0, steps, one, 0)
+        done += steps
+
+
+def flow_kernel(
+    h_in, u_in, v_in, e_in, n_in, f_in, w_in, turning, out,
+    wide, quads1, edge1, side1, quads2, edge2, side2,
+    send1, recv1, send2, recv2,
 ):
-    slope_east = height_rim[2:, 1:-1] - height_rim[:-2, 1:-1]
-    slope_north = height_rim[1:-1, 2:] - height_rim[1:-1, :-2]
-    zonal_new = (
-        FLOW_DAMP * east_flow_component
-        - PRESS_GAIN * slope_east
-        + turning * north_flow_component
-        + WIND_GAIN * stress_east
-    ) * liquid_portion
-    merid_new = (
-        FLOW_DAMP * north_flow_component
-        - PRESS_GAIN * slope_north
-        - turning * zonal_new
-        + WIND_GAIN * stress_north
-    ) * liquid_portion
-    return (zonal_new, merid_new)
-
-
-def height(oceanic_top_sheet, zonal_rim, merid_rim, fresh_in, liquid_portion):
-    spread = (
-        zonal_rim[2:, 1:-1] - zonal_rim[:-2, 1:-1] + (merid_rim[1:-1, 2:] - merid_rim[1:-1, :-2])
-    )
-    return (oceanic_top_sheet - DIVERGE_GAIN * spread - FRESH_GAIN * fresh_in) * liquid_portion
+    fields = (h_in, u_in, v_in, e_in, n_in, f_in, w_in)
+    gains = (None, None, None, WIND_GAIN, WIND_GAIN, FRESH_GAIN, None)
+    greet()
+    for k, (ref, gain) in enumerate(zip(fields, gains)):
+        values = ref[...] if gain is None else gain * ref[...]
+        wide[k, 0, HALF : HALF + OX] = values
+        fill_quads(quads1, k, values)
+    copies = margin_copies(quads1, edge1, side1, send1, recv1)
+    for copy in copies:
+        copy.start()
+    for copy in copies:
+        copy.wait()
+    for k in range(7):
+        spread_margin(edge1, side1, k, wide.at[k])
+    parts = [wide.at[k] for k in range(7)]
+    run_span(*parts, turning)
+    for k in range(3):
+        fill_quads(quads2, k, wide[k, 0, HALF : HALF + OX])
+    copies = margin_copies(quads2, edge2, side2, send2, recv2)
+    for copy in copies:
+        copy.start()
+    for copy in copies:
+        copy.wait()
+    for k in range(3):
+        spread_margin(edge2, side2, k, wide.at[k])
+    run_span(*parts, turning)
+    for k in range(3):
+        out[k] = wide[k, 0, HALF : HALF + OX]
+
+
+def turning_rows():
+    total_y = lax.axis_size("gy") * BAND_NORTH_COUNT
+    lane = jnp.arange(BAND_NORTH_COUNT, dtype=jnp.int32)
+    own = lax.axis_index("gy") * BAND_NORTH_COUNT + lane
+    far = jnp.where(lane < HALF, own + BAND_NORTH_COUNT, own - BAND_NORTH_COUNT)
+    rows = jnp.mod(jnp.stack([own, far]), total_y)
+    return CORIOLIS * jnp.sin(jnp.pi * ((rows.astype(jnp.float32) + 0.5) / total_y - 0.5))
+
+
+def flow(h, u, v, east, north, fresh, wet):
+    def boxes(count):
+        return [
+            pltpu.VMEM((2, 2, count, PACK, BAND_NORTH_COUNT), jnp.bfloat16),
+            pltpu.VMEM((2, 2, count, PACK, BAND_NORTH_COUNT), jnp.bfloat16),
+            pltpu.VMEM((4, 2, count, PACK, BAND_NORTH_COUNT), jnp.bfloat16),
+        ]
+
+    return pl.pallas_call(
+        flow_kernel,
+        out_shape=jax.ShapeDtypeStruct((3, OX, BAND_NORTH_COUNT), jnp.float32),
+        in_specs=[pl.BlockSpec(memory_space=pltpu.VMEM)] * 8,
+        out_specs=pl.BlockSpec(memory_space=pltpu.VMEM),
+        scratch_shapes=[pltpu.VMEM((7, 2, WIDE, BAND_NORTH_COUNT), jnp.float32)]
+        + boxes(7)
+        + boxes(3)
+        + [pltpu.SemaphoreType.DMA((10,))] * 4,
+        compiler_params=pltpu.CompilerParams(collective_id=0, has_side_effects=True),
+        name="flow",
+    )(h, u, v, east, north, fresh, wet, turning_rows())
 
 
 def integrate_scalar_once(
@@ -89,10 +289,6 @@
     tendency = heat_deviation + HORIZ_MIX * horizontal_diffusion + VERT_MIX * vertical
     tendency = tendency.at[0].add(HEAT_GAIN * incoming_enthalpy)
     return tendency * liquid_portion
-
-
-def crop(values, margin):
-    return values[margin : values.shape[0] - margin, margin : values.shape[1] - margin]
 
 
 def per_device(
@@ -187,66 +383,16 @@
     atmo_skin_temp_back = jnp.einsum(
         "nco,no->nc", coupling_matrix_enlarged, skin_mine, preferred_element_type=jnp.float32
     )
-    rim_cells = 2 * DEPTH
-    rows_wide = jnp.mod(
-        lax.axis_index("gy") * BAND_NORTH_COUNT
-        - rim_cells
-        + jnp.arange(BAND_NORTH_COUNT + 2 * rim_cells, dtype=jnp.int32),
-        total_y,
-    )
-    turning_row = CORIOLIS * jnp.sin(
-        jnp.pi * ((rows_wide.astype(jnp.float32) + 0.5) / total_y - 0.5)
-    )
-    turning_wide = jnp.broadcast_to(
-        turning_row[None, :], (OX + 2 * rim_cells, BAND_NORTH_COUNT + 2 * rim_cells)
-    )
-    forcing = padded(
-        jnp.stack(
-            [
-                marine_interface_transfers[0],
-                marine_interface_transfers[1],
-                marine_interface_transfers[3],
-                liquid_portion,
-            ]
-        ),
-        (("gx", 1), ("gy", 2)),
-        rim_cells,
-    )
-
-    def advance_deep(counter, carried):
-        state_wide = padded(jnp.stack(carried), (("gx", 1), ("gy", 2)), rim_cells)
-        oceanic_top_sheet = state_wide[0]
-        east_flow_component = state_wide[1]
-        north_flow_component = state_wide[2]
-        for section_index in range(DEPTH):
-            margin = 2 * section_index + 1
-            east_flow_component, north_flow_component = velocity(
-                oceanic_top_sheet,
-                crop(east_flow_component, 1),
-                crop(north_flow_component, 1),
-                crop(forcing[0], margin),
-                crop(forcing[1], margin),
-                crop(turning_wide, margin),
-                crop(forcing[3], margin),
-            )
-            oceanic_top_sheet = height(
-                crop(oceanic_top_sheet, 2),
-                east_flow_component,
-                north_flow_component,
-                crop(forcing[2], margin + 1),
-                crop(forcing[3], margin + 1),
-            )
-            east_flow_component = crop(east_flow_component, 1)
-            north_flow_component = crop(north_flow_component, 1)
-        return (oceanic_top_sheet, east_flow_component, north_flow_component)
-
-    vertical_mean_flow_answer = lax.fori_loop(
-        0,
-        SUB // DEPTH,
-        advance_deep,
-        (free_marine_lift, depth_averaged_uflow, depth_averaged_vflow),
-    )
-    return (atmo_skin_temp_back, ocean_temp_after_step, jnp.stack(vertical_mean_flow_answer))
+    barotropic = flow(
+        free_marine_lift,
+        depth_averaged_uflow,
+        depth_averaged_vflow,
+        marine_interface_transfers[0],
+        marine_interface_transfers[1],
+        marine_interface_transfers[3],
+        liquid_portion,
+    )
+    return (atmo_skin_temp_back, ocean_temp_after_step, barotropic)
 
 
 def solution(mesh):

time: 339 us -> 99.6 us (0.29)
  waiting for transfers between devices: 119 us -> 0.5 us
  other arithmetic: 92.9 us -> 14.7 us
  starting transfers between devices: 69.8 us -> 23.9 us
  Pallas kernels: 0 us -> 37.2 us
  local copies, waits for them, and re-layouts: 47.6 us -> 15.4 us
    ppermute x24 -> x2, waiting for transfers between devices: 62.8 us -> 0.01 us  [padded(): after = lax.ppermute(first, axis, down)]
    ppermute x24 -> x2, waiting for transfers between devices: 56.2 us -> 0.49 us  [padded(): before = lax.ppermute(last, axis, up)]
    ppermute x24 -> x2, starting transfers between devices: 47.3 us -> 5.08 us  [padded(): after = lax.ppermute(first, axis, down)]
    pallas_call x0 -> x1, Pallas kernels: none -> 37.2 us  [flow(): pl.pallas_call(flow_kernel, out_shape=jax.ShapeDtypeStruct((3, OX, BAND_N...]
    mul x71 -> x1, other arithmetic: 35.7 us -> 0.63 us  [turning_rows(): CORIOLIS * jnp.sin(jnp.pi * ((rows.astype(jnp.float32) + 0.5) / total_y -...]
    concatenate x23 -> x1, other arithmetic: 26.4 us -> 0.88 us  [padded(): x = jnp.concatenate([before, x, after], axis=dim)]
    squeeze x20 -> x0, local copies, waits for them, and re-layouts: 19.2 us -> none  [the longest x10 18.9 us: advance_deep(): forcing[0]]
    slice x11 -> x0, other arithmetic: 10.1 us -> none  [the longest x10 8.59 us: crop(): values[margin:values.shape[0] - margin, margin:values.shape[1] - margin]]
  transfers between devices with their start and end apart: 51 -> 7, of which waited for: 43 -> 1; matrix products, arithmetic and copies ran while one was open for 40% -> 25% of each run, Pallas kernels for 0% -> 38%
where the time goes in v1:
time: 99.6 us; the launch traced here: 98.9 us
  Pallas kernels  37.2 us (37%)
  starting transfers between devices  23.9 us (24%)
  local copies, waits for them, and re-layouts  15.4 us (15%)
  other arithmetic  14.7 us (15%)
  matrix products  6.29 us (6%)
    pallas_call x1, Pallas kernels, flow(): pl.pallas_call(flow_kernel, out_shape=jax.ShapeDtypeStruct((3, OX, BAND_N...  37.2 us
    all_to_all x1, starting transfers between devices, per_device(): lax.all_to_all(packed.reshape(worker_groups, greatest_entries, 4, BAND_NO...  5.95 us
    all_to_all x1, starting transfers between devices, per_device(): lax.all_to_all(rows_sent.reshape(worker_groups, greatest_entries), ('gx',...  5.64 us
    ppermute x2, starting transfers between devices, padded(): after = lax.ppermute(first, axis, down)  5.08 us
    all_to_all x1, starting transfers between devices, per_device(): lax.all_to_all(coupled_skin_warmness_band.reshape(worker_groups, greatest...  4.95 us
    slice x2, local copies, waits for them, and re-layouts, padded(): first = lax.slice_in_dim(x, 0, width, axis=dim)  3.97 us
    add x1, other arithmetic, integrate_scalar_once(): heat_deviation + HORIZ_MIX * horizontal_diffusion + VERT_MIX * vertical  3.94 us
    dot_general x1, matrix products, per_device(): jnp.einsum('nco,no->nc', coupling_matrix_enlarged, skin_mine, preferred_e...  2.35 us
  transfers between devices with their start and end apart: 7, of which 1 were waited for; matrix products, arithmetic and copies ran while one was open for 25% of the time, Pallas kernels for 38%

profile of v1, /device:TPU:0, one launch (start us, length us, event | category | flops | bytes accessed | tf_op | source)
XLA Modules:
  0.0 98.9 jit_solution(10589515964647265444)
XLA Ops:
  0.7 1.0 %fusion.53 = f32[1,128,128]{2,1,0:T(8,128)S(1)} fusion(f32[128]{0:T(128)S(1)} %and_convert_fusion, s32[128,128]{1,0:T(8,128)} %param.15), kind=kLoop, calls=%fused_computation.91 | loop fusion | flops 32768 | bytes 131584 | tf_op jit(solution)/shard_map/broadcast_in_dim | solution.py:355
  1.7 0.8 pad_maximum_fusion.19
  3.0 2.9 %collective-permute-start.1 = (f32[9,1,128]{2,1,0:T(1,128)S(1)}, f32[9,1,128]{2,1,0:T(1,128)S(1)}, u32[]{:S(2)}, u32[]{:S(2)}) collective-permute-start(f32[9,1,128]{2,1,0:T(1,128)S(1)} %get-tuple-element.18), channel_id=1, source_target_pairs={{4,0},{8,4},{12,8},{16,12},{20,16},{24,20},{28,24},{0,28},{5,1},{9... | collective-permute-start | bytes 13832 | tf_op jit(solution)/shard_map/ppermute | solution.py:34
  5.9 0.7 fusion.35
  6.8 0.8 select_reduce_fusion.1
  8.3 0.8 select_reduce_fusion
  9.1 0.7 all_to_all.12
  9.8 5.6 %all-to-all-start = ((s32[32,1,6]{2,1,0:T(1,128)}), s32[32,1,6]{2,1,0:T(1,128)S(1)}, u32[]{:S(2)}, u32[]{:S(2)}) async-start(s32[32,1,6]{2,1,0:T(1,128)} %bitcast.2), calls=%async_computation | async-start | bytes 32768 | tf_op jit(solution)/shard_map/all_to_all | solution.py:335
  15.5 2.2 %fusion.47 = (f32[7,128,128]{2,1,0:T(8,128)}, f32[7,128,128]{2,1,0:T(8,128)}) fusion(f32[8,128,128]{2,1,0:T(8,128)} %param.16), kind=kLoop, calls=%fused_computation.88 | loop fusion | bytes 1835008 | tf_op jit(solution)/shard_map/slice | solution.py:287
  17.7 0.9 fusion.48
  18.6 1.8 %fusion.21 = f32[96,4,128]{2,1,0:T(4,128)S(1)} fusion(bf16[96,128,128]{2,1,0:T(8,128)(2,1)S(1)} %copy-done, bf16[4,96,128]{2,1,0:T(8,128)(2,1)} %param.11), kind=kOutput, calls=%fused_computation.45 | convolution fusion | flops 12582912 | bytes 3440640 | tf_op jit(solution)/shard_map/fnc,nco->nfo/dot_general | solution.py:310
  20.8 1.0 %copy.25 = f32[192,4,128]{2,1,0:T(4,128)} copy(f32[192,4,128]{2,0,1:T(8,128)S(1)} %fusion.18) | data formatting | bytes 786432 | tf_op jit(solution)/shard_map/sn,nfo->sfo/dot_general | solution.py:323
  21.8 0.9 pad_maximum_fusion
  22.7 5.9 %all-to-all-start.1 = ((f32[32,6,4,128]{3,2,1,0:T(4,128)}), f32[32,6,4,128]{3,2,1,0:T(4,128)}, u32[]{:S(2)}, u32[]{:S(2)}) async-start(f32[32,6,4,128]{3,2,1,0:T(4,128)} %bitcast.34), calls=%async_computation.1 | async-start | bytes 786432 | tf_op jit(solution)/shard_map/all_to_all | solution.py:328
  28.6 2.5 %fusion.46 = (f32[9,130,1]{2,1,0:T(8,128)}, f32[9,130,1]{2,1,0:T(8,128)}) fusion(f32[9,130,128]{2,1,0:T(8,128)} %pad_maximum_fusion), kind=kLoop, calls=%fused_computation.87 | loop fusion | bytes 18720 | tf_op jit(solution)/shard_map/slice | solution.py:32
  31.2 1.4 %copy.17 = f32[9,130,1]{1,2,0:T(1,128)S(1)} copy(f32[9,130,1]{2,1,0:T(8,128)} %get-tuple-element.16) | data formatting | bytes 9360 | tf_op jit(solution)/shard_map/slice | solution.py:31
  32.6 1.7 %collective-permute-start.2 = (f32[9,130,1]{1,2,0:T(1,128)S(1)}, f32[9,130,1]{1,2,0:T(1,128)S(1)}, u32[]{:S(2)}, u32[]{:S(2)}) collective-permute-start(f32[9,130,1]{1,2,0:T(1,128)S(1)} %copy.17), channel_id=1, source_target_pairs={{0,1},{1,2},{2,3},{3,0},{4,5},{5,6},{6,7},{7,4},{8,9},{9,10},{10,1... | collective-permute-start | bytes 14048 | tf_op jit(solution)/shard_map/ppermute | solution.py:33
  34.3 1.4 %copy.18 = f32[9,130,1]{1,2,0:T(1,128)S(1)} copy(f32[9,130,1]{2,1,0:T(8,128)} %get-tuple-element.15) | data formatting | bytes 9360 | tf_op jit(solution)/shard_map/slice | solution.py:32
  35.8 2.1 %collective-permute-start.3 = (f32[9,130,1]{1,2,0:T(1,128)S(1)}, f32[9,130,1]{1,2,0:T(1,128)S(1)}, u32[]{:S(2)}, u32[]{:S(2)}) collective-permute-start(f32[9,130,1]{1,2,0:T(1,128)S(1)} %copy.18), channel_id=1, source_target_pairs={{1,0},{2,1},{3,2},{0,3},{5,4},{6,5},{7,6},{4,7},{9,8},{10,9},{11,1... | collective-permute-start | bytes 14048 | tf_op jit(solution)/shard_map/ppermute | solution.py:34
  38.4 0.7 reduce.5
  39.7 1.1 %copy.19 = f32[9,130,1]{2,1,0:T(8,128)} copy(f32[9,130,1]{1,2,0:T(1,128)S(1)} %collective-permute-done.2) | data formatting | bytes 9360 | tf_op jit(solution)/shard_map/ppermute | solution.py:33
  40.8 1.1 %copy.20 = f32[9,130,1]{2,1,0:T(8,128)} copy(f32[9,130,1]{1,2,0:T(1,128)S(1)} %collective-permute-done.3) | data formatting | bytes 9360 | tf_op jit(solution)/shard_map/ppermute | solution.py:34
  42.0 1.0 %fusion.20 = f32[130,130]{1,0:T(8,128)S(1)} fusion(f32[9,130,1]{2,1,0:T(8,128)} %copy.20, f32[9,130,1]{2,1,0:T(8,128)} %copy.19, f32[9,1,128]{2,1,0:T(1,128)S(1)} %collective-permute-done.1, f32[9,1,128]{2,1,0:T(1,128)S(1)} %collective-permute-done, f32[1,128,128]{2,1,0:T(8,128)S(1)} %fusion.53, f32[8,128,128]{2,1,0:T(8,128)} %param.16), kind=kLoop, calls=%fused_computation.40 | loop fusion | flops 84500 | bytes 676000 | tf_op jit(solution)/shard_map/squeeze | solution.py:360
  43.1 3.9 %fusion.6 = f32[8,128,128]{2,1,0:T(8,128)} fusion(f32[8,128,128]{2,1,0:T(8,128)} %param.16, f32[9,130,1]{2,1,0:T(8,128)} %copy.19, f32[9,1,128]{2,1,0:T(1,128)S(1)} %collective-permute-done.1, f32[9,1,128]{2,1,0:T(1,128)S(1)} %collective-permute-done, f32[1,128,128]{2,1,0:T(8,128)S(1)} %fusion.53, f32[9,130,1]{2,1,0:T(8,128)} %copy.20, ...), kind=kLoop, calls=%fused_computation.11 | loop fusion | flops 4194304 | bytes 2443408 | tf_op jit(solution)/shard_map/add | solution.py:289
  47.1 1.4 %convolution_bitcast_fusion = f32[4,128,128]{2,1,0:T(8,128)S(1)} fusion(f32[192,4,128]{2,1,0:T(4,128)} %bitcast.7, s32[192]{0:T(256)S(1)} %eq.49), kind=kOutput, calls=%fused_computation | convolution fusion | flops 151019520 | bytes 656128 | tf_op jit(solution)/shard_map/sx,sfo->fxo/dot_general | solution.py:346
  48.4 1.5 %slice_bitcast_fusion = (f32[128,128]{1,0:T(8,128)}, f32[128,128]{1,0:T(8,128)}, f32[128,128]{1,0:T(8,128)}, f32[8,128,128]{2,1,0:T(8,128)}) fusion(f32[4,128,128]{2,1,0:T(8,128)S(1)} %convolution_bitcast_fusion, f32[8,128,128]{2,1,0:T(8,128)} %fusion.6), kind=kLoop, calls=%fused_computation.52 | loop fusion | flops 32768 | bytes 589824 | tf_op jit(solution)/shard_map/squeeze | solution.py:392
  50.0 1.1 %broadcast_multiply_fusion = f32[8,128,128]{2,1,0:T(8,128)S(1)} fusion(f32[8,128,128]{2,1,0:T(8,128)} %get-tuple-element.26, f32[128,128]{1,0:T(8,128)S(1)} %convert_multiply_fusion.w_in), kind=kLoop, calls=%fused_computation.36 | loop fusion | flops 131072 | bytes 1114112 | tf_op jit(solution)/shard_map/mul | solution.py:291
  51.1 0.8 copy-done.3
  52.7 4.9 %all-to-all-start.2 = ((bf16[32,6,128]{2,1,0:T(8,128)(2,1)}), bf16[32,6,128]{2,1,0:T(8,128)(2,1)S(1)}, u32[]{:S(2)}, u32[]{:S(2)}) async-start(bf16[32,6,128]{2,1,0:T(8,128)(2,1)} %reshape.102), calls=%async_computation.2 | async-start | bytes 131072 | tf_op jit(solution)/shard_map/all_to_all | solution.py:370
  58.3 37.2 %flow.1 = f32[3,128,128]{2,1,0:T(8,128)} custom-call(f32[128,128]{1,0:T(8,128)} %h_in.1, f32[128,128]{1,0:T(8,128)} %u_in.1, f32[128,128]{1,0:T(8,128)} %v_in.1, f32[128,128]{1,0:T(8,128)} %get-tuple-element.25.e_in, f32[128,128]{1,0:T(8,128)} %get-tuple-element.24.n_in, f32[128,128]{1,0:T(8,128)} %get-tuple-element.23.f_in, f32[128,128]{1,0:T(8,128)} %copy-done.4, ...), custom_call_target="tpu_custom_call" | custom-call | tf_op jit(solution)/shard_map/flow/pallas_call | solution.py:257
  95.8 2.4 %fusion.29 = f32[96,1,128]{2,1,0:T(1,128)} fusion(bf16[96,128,128]{2,1,0:T(8,128)(2,1)S(1)} %copy-done, bf16[96,128,1]{1,0,2:T(8,128)(2,1)S(1)} %fusion), kind=kOutput, calls=%fused_computation.60 | convolution fusion | flops 3145728 | bytes 3219456 | tf_op jit(solution)/shard_map/nco,no->nc/dot_general | solution.py:383
  98.2 0.7 copy.41
  (33 shorter events, 4.7 us)
Async XLA Ops:
  0.6 18.0 %copy-start = (bf16[96,128,128]{2,1,0:T(8,128)(2,1)S(1)}, bf16[96,128,128]{2,1,0:T(8,128)(2,1)}, u32[]{:S(2)}) copy-start(bf16[96,128,128]{2,1,0:T(8,128)(2,1)} %param.12) | copy-start | bytes 9437188
  2.4 19.3 %collective-permute-start = (f32[9,1,128]{2,1,0:T(1,128)S(1)}, f32[9,1,128]{2,1,0:T(1,128)S(1)}, u32[]{:S(2)}, u32[]{:S(2)}) collective-permute-start(f32[9,1,128]{2,1,0:T(1,128)S(1)} %get-tuple-element.17), channel_id=1, source_target_pairs={{0,4},{4,8},{8,12},{12,16},{16,20},{20,24},{24,28},{28,0},{1,5},{5... | collective-permute-start | bytes 13832 | tf_op jit(solution)/shard_map/ppermute | solution.py:33
  3.0 18.8 %collective-permute-start.1 = (f32[9,1,128]{2,1,0:T(1,128)S(1)}, f32[9,1,128]{2,1,0:T(1,128)S(1)}, u32[]{:S(2)}, u32[]{:S(2)}) collective-permute-start(f32[9,1,128]{2,1,0:T(1,128)S(1)} %get-tuple-element.18), channel_id=1, source_target_pairs={{4,0},{8,4},{12,8},{16,12},{20,16},{24,20},{28,24},{0,28},{5,1},{9... | collective-permute-start | bytes 13832 | tf_op jit(solution)/shard_map/ppermute | solution.py:34
  6.7 14.1 %copy-start.5 = (s32[128,128]{1,0:T(8,128)S(1)}, s32[128,128]{1,0:T(8,128)}, u32[]{:S(2)}) copy-start(s32[128,128]{1,0:T(8,128)} %param.15) | copy-start | bytes 196612
  9.8 12.9 %all-to-all-start = ((s32[32,1,6]{2,1,0:T(1,128)}), s32[32,1,6]{2,1,0:T(1,128)S(1)}, u32[]{:S(2)}, u32[]{:S(2)}) async-start(s32[32,1,6]{2,1,0:T(1,128)} %bitcast.2), calls=%async_computation | async-start | bytes 32768 | tf_op jit(solution)/shard_map/all_to_all | solution.py:335
  15.5 6.3 %copy-start.1 = (f32[8,128,128]{2,1,0:T(8,128)S(1)}, f32[8,128,128]{2,1,0:T(8,128)}, u32[]{:S(2)}) copy-start(f32[8,128,128]{2,1,0:T(8,128)} %param.16) | copy-start | bytes 1572868
  20.8 29.2 %copy-start.4 = (f32[128,128]{1,0:T(8,128)}, f32[128,128]{1,0:T(8,128)S(1)}, u32[]{:S(2)}) copy-start(f32[128,128]{1,0:T(8,128)S(1)} %convert_multiply_fusion.w_in) | copy-start | bytes 196612
  22.7 24.4 %all-to-all-start.1 = ((f32[32,6,4,128]{3,2,1,0:T(4,128)}), f32[32,6,4,128]{3,2,1,0:T(4,128)}, u32[]{:S(2)}, u32[]{:S(2)}) async-start(f32[32,6,4,128]{3,2,1,0:T(4,128)} %bitcast.34), calls=%async_computation.1 | async-start | bytes 786432 | tf_op jit(solution)/shard_map/all_to_all | solution.py:328
  32.6 7.1 %collective-permute-start.2 = (f32[9,130,1]{1,2,0:T(1,128)S(1)}, f32[9,130,1]{1,2,0:T(1,128)S(1)}, u32[]{:S(2)}, u32[]{:S(2)}) collective-permute-start(f32[9,130,1]{1,2,0:T(1,128)S(1)} %copy.17), channel_id=1, source_target_pairs={{0,1},{1,2},{2,3},{3,0},{4,5},{5,6},{6,7},{7,4},{8,9},{9,10},{10,1... | collective-permute-start | bytes 14048 | tf_op jit(solution)/shard_map/ppermute | solution.py:33
  35.8 5.1 %collective-permute-start.3 = (f32[9,130,1]{1,2,0:T(1,128)S(1)}, f32[9,130,1]{1,2,0:T(1,128)S(1)}, u32[]{:S(2)}, u32[]{:S(2)}) collective-permute-start(f32[9,130,1]{1,2,0:T(1,128)S(1)} %copy.18), channel_id=1, source_target_pairs={{1,0},{2,1},{3,2},{0,3},{5,4},{6,5},{7,6},{4,7},{9,8},{10,9},{11,1... | collective-permute-start | bytes 14048 | tf_op jit(solution)/shard_map/ppermute | solution.py:34
  51.1 0.8 copy-start.3
  52.7 42.8 %all-to-all-start.2 = ((bf16[32,6,128]{2,1,0:T(8,128)(2,1)}), bf16[32,6,128]{2,1,0:T(8,128)(2,1)S(1)}, u32[]{:S(2)}, u32[]{:S(2)}) async-start(bf16[32,6,128]{2,1,0:T(8,128)(2,1)} %reshape.102), calls=%async_computation.2 | async-start | bytes 131072 | tf_op jit(solution)/shard_map/all_to_all | solution.py:370
  95.6 2.6 %copy-start.2 = (f32[3,128,128]{2,1,0:T(8,128)S(1)}, f32[3,128,128]{2,1,0:T(8,128)}, u32[]{:S(2)}) copy-start(f32[3,128,128]{2,1,0:T(8,128)} %flow.1) | copy-start | bytes 589828

commit v2 on v1

v2 whole, which is shorter than its diff:
```python
import jax
import jax.numpy as jnp
from jax import lax
from jax.experimental import pallas as pl
from jax.experimental.pallas import tpu as pltpu
from jax.sharding import PartitionSpec as P

NB = 96
OX = 128
BAND_NORTH_COUNT = 128
MARINE_STRATA = 8
SUB = 40


HORIZ_MIX = 0.15
VERT_MIX = 0.2
HEAT_GAIN = 0.5
FLOW_DAMP = 0.98
PRESS_GAIN = 0.6
DIVERGE_GAIN = 0.6
CORIOLIS = 0.1
WIND_GAIN = 0.05
FRESH_GAIN = 0.05


MESH = pl.DeviceIdType.MESH
HALF = BAND_NORTH_COUNT // 2
WIDE = OX + 2 * HALF
PACK = HALF // 2
SPAN = SUB // 2
CHUNK = 16
SLOTS = 8


def low_lanes(rows):
    return lax.broadcasted_iota(jnp.int32, (rows, BAND_NORTH_COUNT), 1) < HALF


def pack_half(values):
    low = low_lanes(PACK)
    first, second = values[:PACK], pltpu.roll(values[PACK:], HALF, 1)
    return (
        jnp.where(low, first, second).astype(jnp.bfloat16),
        jnp.where(low, second, first).astype(jnp.bfloat16),
    )


def unpack_half(low_quadrant, high_quadrant):
    low = low_lanes(PACK)
    lo = low_quadrant.astype(jnp.float32)
    hi = high_quadrant.astype(jnp.float32)
    return jnp.where(low, lo, hi), pltpu.roll(jnp.where(low, hi, lo), HALF, 1)


def neighbours():
    nx, ny = lax.axis_size("gx"), lax.axis_size("gy")
    x, y = lax.axis_index("gx"), lax.axis_index("gy")
    up, down = lax.rem(x + 1, nx), lax.rem(x + nx - 1, nx)
    right, left = lax.rem(y + 1, ny), lax.rem(y + ny - 1, ny)
    return x, y, up, down, right, left


def peer_place(index):
    ny = lax.axis_size("gy")
    return lax.div(index, ny), lax.rem(index, ny)


def greet_all(me, count):
    barrier = pltpu.get_barrier_semaphore()

    def one(k, carry):
        place = peer_place(lax.rem(me + k, count))
        pl.semaphore_signal(barrier, inc=1, device_id=place, device_id_type=MESH)
        return carry

    lax.fori_loop(1, count, one, 0)


def swap_all(action, me, count, out, into, send_sem, recv_sem):
    def one(k, carry):
        peer = lax.rem(me + k, count)
        copy = pltpu.make_async_remote_copy(
            src_ref=out.at[peer],
            dst_ref=into.at[me],
            send_sem=send_sem.at[k],
            recv_sem=recv_sem.at[k],
            device_id=peer_place(peer),
            device_id_type=MESH,
        )
        if action == "start":
            copy.start()
        else:
            copy.wait()
        return carry

    lax.fori_loop(1, count, one, 0)


def as_bits(condition):
    return jnp.where(condition, 1.0, 0.0).astype(jnp.bfloat16)


def line_numbers(shape, axis):
    return lax.broadcasted_iota(jnp.int32, shape, axis).astype(jnp.float32)


def dot(a, b, a_dim=1, b_dim=0):
    return lax.dot_general(
        a, b, (((a_dim,), (b_dim,)), ((), ())), preferred_element_type=jnp.float32
    )


def place_blocks(keeper, lines, count):
    i, j = line_numbers((NB, NB), 0), line_numbers((NB, NB), 1)
    owner_col = keeper[...].astype(jnp.float32)
    owner_row = jnp.sum(jnp.where(i == j, owner_col, 0.0), axis=0, keepdims=True)
    same = jnp.where(owner_col == owner_row, 1.0, 0.0)
    rank_row = jnp.sum(jnp.where(i < j, same, 0.0), axis=0, keepdims=True)
    rank_col = jnp.sum(jnp.where(j < i, same, 0.0), axis=1, keepdims=True)
    line_row = lines[...].astype(jnp.float32)
    line_col = jnp.sum(jnp.where(i == j, line_row, 0.0), axis=1, keepdims=True)
    hot = as_bits(line_numbers((NB, OX), 1) == line_col)
    key_row = owner_row * SLOTS + rank_row
    key_col = owner_col * SLOTS + rank_col
    return key_row, rank_row, key_col, hot


def fill_send(send, partial, key_row, rank_row, hot, count, most):
    spare = SLOTS - most
    place = line_numbers((count * SLOTS, NB), 0)
    slots = as_bits(place == key_row)
    out = []
    for f in range(4):
        value = dot(slots, partial[f].astype(jnp.bfloat16))
        if f * spare < most:
            here = (rank_row >= f * spare) & (rank_row < (f + 1) * spare)
            spot = jnp.where(here, key_row - f * spare + most, -1.0)
            value = value + dot(as_bits(place == spot), hot)
        out.append(value.reshape(count, SLOTS, BAND_NORTH_COUNT))
    for p in range(2):
        both = jnp.concatenate([out[2 * p], out[2 * p + 1]], axis=1)
        send[:, 2 * SLOTS * p : 2 * SLOTS * (p + 1), :] = both.astype(jnp.bfloat16)


def read_received(recv, count, most):
    spare = SLOTS - most
    total = count * SLOTS
    values = []
    for p in range(2):
        both = recv[:, 2 * SLOTS * p : 2 * SLOTS * (p + 1), :].astype(jnp.float32)
        values.append(both[:, :SLOTS].reshape(total, BAND_NORTH_COUNT))
        values.append(both[:, SLOTS:].reshape(total, BAND_NORTH_COUNT))
    slot = lax.broadcasted_iota(jnp.int32, (count, SLOTS, BAND_NORTH_COUNT), 1)
    slot = slot.reshape(total, BAND_NORTH_COUNT)
    target = jnp.zeros((total, BAND_NORTH_COUNT), jnp.float32)
    for f in range(4):
        if f * spare < most:
            moved = pltpu.roll(values[f], total - (most - f * spare), 0)
            here = (slot >= f * spare) & (slot < min((f + 1) * spare, most))
            target = jnp.where(here, moved, target)
    return [value.astype(jnp.bfloat16) for value in values], target


def edge_selector(rows, low_row, high_row):
    row = lax.broadcasted_iota(jnp.int32, (rows, BAND_NORTH_COUNT), 0)
    lane = lax.broadcasted_iota(jnp.int32, (rows, BAND_NORTH_COUNT), 1)
    return as_bits(
        ((row == low_row) & (lane == 0)) | ((row == high_row) & (lane == BAND_NORTH_COUNT - 1))
    )


def fill_heat_edges(heat, edges):
    selector = edge_selector(8, 0, 1)
    for k in range(MARINE_STRATA):
        level = slice(k, k + 1)
        edges[0, level] = heat[k, 0:1]
        edges[1, level] = heat[k, OX - 1 : OX]
        sides = dot(selector, heat[k].astype(jnp.bfloat16), 1, 1)
        edges[2, level] = sides[0:1]
        edges[3, level] = sides[1:2]


def heat_copies(edges, got, send_sem, recv_sem):
    x, y, up, down, right, left = neighbours()
    plan = ((1, 0, (up, y)), (0, 1, (down, y)), (3, 2, (x, right)), (2, 3, (x, left)))
    return [
        pltpu.make_async_remote_copy(
            src_ref=edges.at[src],
            dst_ref=got.at[dst],
            send_sem=send_sem.at[k],
            recv_sem=recv_sem.at[k],
            device_id=place,
            device_id_type=MESH,
        )
        for k, (src, dst, place) in enumerate(plan)
    ]


def heat_step(heat, got, tall, wet, near, out):
    own = slice(HALF, HALF + OX)
    last = lax.broadcasted_iota(jnp.int32, (OX, BAND_NORTH_COUNT), 1) == BAND_NORTH_COUNT - 1
    first = lax.broadcasted_iota(jnp.int32, (OX, BAND_NORTH_COUNT), 1) == 0
    mine, far = wet[0, own], wet[1, own]
    near[0] = jnp.where(last, pltpu.roll(far, OX - 1, 1), pltpu.roll(mine, OX - 1, 1))
    near[1] = jnp.where(first, pltpu.roll(far, 1, 1), pltpu.roll(mine, 1, 1))
    sides = jnp.concatenate([got[3], got[2]], axis=0).astype(jnp.bfloat16)
    for k in range(MARINE_STRATA):
        tall[k, 8 : 8 + OX] = heat[k]
        tall[k, 7:8] = got[0, k : k + 1]
        tall[k, 8 + OX : 9 + OX] = got[1, k : k + 1]
        near[2 + k] = dot(sides, edge_selector(2 * MARINE_STRATA, MARINE_STRATA + k, k), 0, 0)

    step = 32
    last, first = last[:step], first[:step]

    def one(k, carry):
        above, below = jnp.maximum(k - 1, 0), jnp.minimum(k + 1, MARINE_STRATA - 1)
        for start in range(0, OX, step):
            rows = slice(start, start + step)
            wide_rows = lambda shift: slice(HALF + start + shift, HALF + start + step + shift)
            here = heat[k, rows]
            side = near[2 + k, rows]
            north = jnp.where(last, side, pltpu.roll(here, OX - 1, 1))
            south = jnp.where(first, side, pltpu.roll(here, 1, 1))
            lateral = wet[0, wide_rows(1)] * (tall[k, 9 + start : 9 + start + step] - here)
            lateral = lateral + wet[0, wide_rows(-1)] * (
                tall[k, 7 + start : 7 + start + step] - here
            )
            lateral = lateral + near[0, rows] * (north - here)
            lateral = lateral + near[1, rows] * (south - here)
            vertical = (heat[above, rows] - here) + (heat[below, rows] - here)
            out[k, rows] = (here + HORIZ_MIX * lateral + VERT_MIX * vertical) * wet[0, wide_rows(0)]
        return carry

    lax.fori_loop(0, MARINE_STRATA, one, 0)


def margin_copies(quads, edge, side, send_sem, recv_sem):
    x, y, up, down, right, left = neighbours()
    plan = (
        (quads.at[1], edge.at[0], (up, y)),
        (quads.at[0], edge.at[1], (down, y)),
        (quads.at[0, 1], side.at[1, 1], (x, right)),
        (quads.at[1, 1], side.at[2, 1], (x, right)),
        (quads.at[0, 0], side.at[1, 0], (x, left)),
        (quads.at[1, 0], side.at[2, 0], (x, left)),
        (quads.at[1, 1], side.at[0, 1], (up, right)),
        (quads.at[1, 0], side.at[0, 0], (up, left)),
        (quads.at[0, 1], side.at[3, 1], (down, right)),
        (quads.at[0, 0], side.at[3, 0], (down, left)),
    )
    return [
        pltpu.make_async_remote_copy(
            src_ref=src,
            dst_ref=dst,
            send_sem=send_sem.at[k],
            recv_sem=recv_sem.at[k],
            device_id=place,
            device_id_type=MESH,
        )
        for k, (src, dst, place) in enumerate(plan)
    ]


def fill_quads(quads, field, values):
    for part in range(2):
        lo, hi = pack_half(values[part * HALF : (part + 1) * HALF])
        quads[part, 0, field] = lo
        quads[part, 1, field] = hi


def spread_margin(edge, side, field, wide):
    for row_block in range(4):
        start = row_block * HALF
        if row_block in (0, 3):
            at = 0 if row_block == 0 else 1
            one, two = unpack_half(edge[at, 0, field], edge[at, 1, field])
            wide[0, start : start + PACK] = one
            wide[0, start + PACK : start + HALF] = two
        one, two = unpack_half(side[row_block, 0, field], side[row_block, 1, field])
        wide[1, start : start + PACK] = one
        wide[1, start + PACK : start + HALF] = two


def lat_difference(own, far):
    lane = lax.broadcasted_iota(jnp.int32, own.shape, 1)
    last, first = lane == BAND_NORTH_COUNT - 1, lane == 0
    own_up = pltpu.roll(own, BAND_NORTH_COUNT - 1, 1)
    far_up = pltpu.roll(far, BAND_NORTH_COUNT - 1, 1)
    own_down = pltpu.roll(own, 1, 1)
    far_down = pltpu.roll(far, 1, 1)
    return (
        jnp.where(last, far_up, own_up) - jnp.where(first, far_down, own_down),
        jnp.where(last, own_up, far_up) - jnp.where(first, own_down, far_down),
    )


def substep(reach, h, u, v, east, north, fresh, wet, turning):
    low, high = HALF - reach, HALF + OX + reach
    turn = [
        jnp.broadcast_to(turning[tile : tile + 1, :], (CHUNK, BAND_NORTH_COUNT))
        for tile in range(2)
    ]
    for start in range(low, high, CHUNK):
        rows = slice(start, start + CHUNK)
        slope_north = lat_difference(h[0, rows], h[1, rows])
        for tile in range(2):
            slope_east = (
                h[tile, start + 1 : start + CHUNK + 1] - h[tile, start - 1 : start + CHUNK - 1]
            )
            old_u, old_v, mask = u[tile, rows], v[tile, rows], wet[tile, rows]
            new_u = (
                FLOW_DAMP * old_u - PRESS_GAIN * slope_east + turn[tile] * old_v + east[tile, rows]
            ) * mask
            u[tile, rows] = new_u
            v[tile, rows] = (
                FLOW_DAMP * old_v
                - PRESS_GAIN * slope_north[tile]
                - turn[tile] * new_u
                + north[tile, rows]
            ) * mask
    for start in range(low, high, CHUNK):
        rows = slice(start, start + CHUNK)
        spread_north = lat_difference(v[0, rows], v[1, rows])
        for tile in range(2):
            spread_east = (
                u[tile, start + 1 : start + CHUNK + 1] - u[tile, start - 1 : start + CHUNK - 1]
            )
            h[tile, rows] = (
                h[tile, rows]
                - DIVERGE_GAIN * (spread_east + spread_north[tile])
                - fresh[tile, rows]
            ) * wet[tile, rows]


def run_span(h, u, v, east, north, fresh, wet, turning):
    done = 0
    while done < SPAN:
        need = 2 * (SPAN - done) - 1
        reach = -(-need // 8) * 8
        steps = min(SPAN - done, 4)

        def one(_, carry, reach=reach):
            substep(reach, h, u, v, east, north, fresh, wet, turning)
            return carry

        lax.fori_loop(0, steps, one, 0)
        done += steps


def window_kernel(
    sky, weights_far, keeper, lines, sea, heat, h_in, u_in, v_in, turning,
    back, heat_out, out,
    weights, sky32, partial, send, recv, skin_send, skin_recv,
    heat_edges, heat_got, tall, near,
    wide, quads1, edge1, side1, quads2, edge2, side2, quads3, edge3, side3,
    load_sem, a2a_send, a2a_recv, skin_send_sem, skin_recv_sem,
    heat_send_sem, heat_recv_sem, send1, recv1, send2, recv2, send3, recv3,
):
    ny = lax.axis_size("gy")
    count = lax.axis_size("gx") * ny
    most = max(2, 2 * NB // count)
    me = lax.axis_index("gx") * ny + lax.axis_index("gy")
    own = slice(HALF, HALF + OX)
    greet_all(me, count)
    load = pltpu.make_async_copy(weights_far, weights, load_sem)
    load.start()
    lat = lax.axis_index("gy") * BAND_NORTH_COUNT + lax.broadcasted_iota(
        jnp.int32, (OX, BAND_NORTH_COUNT), 1
    )
    inside = (lat > 0) & (lat < ny * BAND_NORTH_COUNT - 1)
    mask = jnp.where(inside, sea[...].astype(jnp.float32), 0.0)
    for k, values in enumerate((h_in[...], u_in[...], v_in[...], mask)):
        wide[k, 0, own] = values
        fill_quads(quads1, k, values)
    fill_heat_edges(heat, heat_edges)
    sky32[...] = sky[...].astype(jnp.float32)
    key_row, rank_row, key_col, hot = place_blocks(keeper, lines, count)
    pl.semaphore_wait(pltpu.get_barrier_semaphore(), count - 1)
    copies1 = margin_copies(quads1, edge1, side1, send1, recv1)
    heats = heat_copies(heat_edges, heat_got, heat_send_sem, heat_recv_sem)
    for copy in copies1 + heats:
        copy.start()
    load.wait()
    slot32 = lax.rem(
        lax.broadcasted_iota(jnp.int32, (4 * SLOTS, BAND_NORTH_COUNT), 0), SLOTS
    )
    for g in range(NB // SLOTS):
        rows = slice(g * SLOTS, (g + 1) * SLOTS)
        fluxes = sky32[:, rows, :].reshape(4 * SLOTS, OX).astype(jnp.bfloat16)
        total = dot(fluxes, weights[g * SLOTS])
        for n in range(1, SLOTS):
            total = jnp.where(slot32 == n, dot(fluxes, weights[g * SLOTS + n]), total)
        partial[:, rows, :] = total.reshape(4, SLOTS, BAND_NORTH_COUNT)
    fill_send(send, partial, key_row, rank_row, hot, count, most)
    swap_all("start", me, count, send, recv, a2a_send, a2a_recv)
    recv[me] = send[me]
    for copy in copies1 + heats:
        copy.wait()
    for k in range(4):
        spread_margin(edge1, side1, k, wide.at[k])
    heat_step(heat, heat_got, tall, wide.at[3], near, heat_out)
    swap_all("wait", me, count, send, recv, a2a_send, a2a_recv)
    values, target = read_received(recv, count, most)
    target_turned = target.T.astype(jnp.bfloat16)
    target = target.astype(jnp.bfloat16)
    for k, (f, gain) in enumerate(((0, WIND_GAIN), (1, WIND_GAIN), (3, FRESH_GAIN))):
        flux = gain * dot(target_turned, values[f])
        wide[4 + k, 0, own] = flux
        fill_quads(quads2, k, flux)
    copies2 = margin_copies(quads2, edge2, side2, send2, recv2)
    for copy in copies2:
        copy.start()
    surface = heat_out[0] + HEAT_GAIN * dot(target_turned, values[2]) * wide[3, 0, own]
    heat_out[0] = surface
    band = dot(target, surface.astype(jnp.bfloat16))
    skin_send[...] = band.reshape(count, SLOTS, BAND_NORTH_COUNT)
    swap_all("start", me, count, skin_send, skin_recv, skin_send_sem, skin_recv_sem)
    skin_recv[me] = skin_send[me]
    for copy in copies2:
        copy.wait()
    for k in range(3):
        spread_margin(edge2, side2, k, wide.at[4 + k])
    parts = [wide.at[k] for k in (0, 1, 2, 4, 5, 6, 3)]
    run_span(*parts, turning)
    for k in range(3):
        fill_quads(quads3, k, wide[k, 0, own])
    copies3 = margin_copies(quads3, edge3, side3, send3, recv3)
    for copy in copies3:
        copy.start()
    swap_all("wait", me, count, skin_send, skin_recv, skin_send_sem, skin_recv_sem)
    slots = as_bits(line_numbers((NB, count * SLOTS), 1) == key_col)
    skin = dot(slots, skin_recv[...].reshape(count * SLOTS, BAND_NORTH_COUNT).astype(jnp.bfloat16))
    slot8 = lax.broadcasted_iota(jnp.int32, (SLOTS, BAND_NORTH_COUNT), 0)
    for g in range(NB // SLOTS):
        rows = slice(g * SLOTS, (g + 1) * SLOTS)
        lines_skin = skin[rows].astype(jnp.bfloat16)
        total = dot(lines_skin, weights[g * SLOTS], 1, 1)
        for n in range(1, SLOTS):
            total = jnp.where(slot8 == n, dot(lines_skin, weights[g * SLOTS + n], 1, 1), total)
        back[rows] = total
    for copy in copies3:
        copy.wait()
    for k in range(3):
        spread_margin(edge3, side3, k, wide.at[k])
    run_span(*parts, turning)
    for k in range(3):
        out[k] = wide[k, 0, own]


def turning_rows():
    total_y = lax.axis_size("gy") * BAND_NORTH_COUNT
    lane = jnp.arange(BAND_NORTH_COUNT, dtype=jnp.int32)
    own = lax.axis_index("gy") * BAND_NORTH_COUNT + lane
    far = jnp.where(lane < HALF, own + BAND_NORTH_COUNT, own - BAND_NORTH_COUNT)
    rows = jnp.mod(jnp.stack([own, far]), total_y)
    return CORIOLIS * jnp.sin(jnp.pi * ((rows.astype(jnp.float32) + 0.5) / total_y - 0.5))


def per_device(
    sky_interface_transfers,
    coupling_matrix_enlarged,
    piece_keeper_part,
    receiving_part_line,
    marine_point_switch,
    potential_heat_deviation,
    free_marine_lift,
    depth_averaged_uflow,
    depth_averaged_vflow,
):
    count = lax.axis_size("gx") * lax.axis_size("gy")
    line = BAND_NORTH_COUNT

    def boxes(fields):
        return [
            pltpu.VMEM((2, 2, fields, PACK, line), jnp.bfloat16),
            pltpu.VMEM((2, 2, fields, PACK, line), jnp.bfloat16),
            pltpu.VMEM((4, 2, fields, PACK, line), jnp.bfloat16),
        ]

    inside = pl.BlockSpec(memory_space=pltpu.VMEM)
    return pl.pallas_call(
        window_kernel,
        out_shape=(
            jax.ShapeDtypeStruct((NB, OX), jnp.float32),
            jax.ShapeDtypeStruct((MARINE_STRATA, OX, line), jnp.float32),
            jax.ShapeDtypeStruct((3, OX, line), jnp.float32),
        ),
        in_specs=[inside, pl.BlockSpec(memory_space=pl.ANY)] + [inside] * 8,
        out_specs=(inside,) * 3,
        scratch_shapes=[
            pltpu.VMEM((NB, OX, line), jnp.bfloat16),
            pltpu.VMEM((4, NB, OX), jnp.float32),
            pltpu.VMEM((4, NB, line), jnp.float32),
            pltpu.VMEM((count, 4 * SLOTS, line), jnp.bfloat16),
            pltpu.VMEM((count, 4 * SLOTS, line), jnp.bfloat16),
            pltpu.VMEM((count, SLOTS, line), jnp.float32),
            pltpu.VMEM((count, SLOTS, line), jnp.float32),
            pltpu.VMEM((4, MARINE_STRATA, line), jnp.float32),
            pltpu.VMEM((4, MARINE_STRATA, line), jnp.float32),
            pltpu.VMEM((MARINE_STRATA, OX + 16, line), jnp.float32),
            pltpu.VMEM((2 + MARINE_STRATA, OX, line), jnp.float32),
            pltpu.VMEM((7, 2, WIDE, line), jnp.float32),
        ]
        + boxes(4)
        + boxes(3)
        + boxes(3)
        + [pltpu.SemaphoreType.DMA]
        + [pltpu.SemaphoreType.DMA((count,))] * 4
        + [pltpu.SemaphoreType.DMA((4,))] * 2
        + [pltpu.SemaphoreType.DMA((10,))] * 6,
        compiler_params=pltpu.CompilerParams(collective_id=0, has_side_effects=True),
        name="window",
    )(
        sky_interface_transfers,
        coupling_matrix_enlarged,
        piece_keeper_part.reshape(NB, 1),
        receiving_part_line,
        marine_point_switch,
        potential_heat_deviation,
        free_marine_lift,
        depth_averaged_uflow,
        depth_averaged_vflow,
        turning_rows(),
    )


def solution(mesh):
    in_specs = (
        P(None, "gy", "gx"),
        P("gy", "gx", None),
        P("gx", "gy", None),
        P("gx", "gy"),
        P("gx", "gy"),
        P(None, "gx", "gy"),
        P("gx", "gy"),
        P("gx", "gy"),
        P("gx", "gy"),
    )
    out_specs = (P("gy", "gx"), P(None, "gx", "gy"), P(None, "gx", "gy"))
    return jax.shard_map(
        per_device, mesh=mesh, in_specs=in_specs, out_specs=out_specs, check_vma=False
    )
```

time: 99.6 us -> 57.2 us (0.57)
  starting transfers between devices: 23.9 us -> 0 us
  other arithmetic: 14.7 us -> 0.63 us
  Pallas kernels: 37.2 us -> 49.4 us
  local copies, waits for them, and re-layouts: 15.4 us -> 6.28 us
  matrix products: 6.29 us -> 0 us
    all_to_all x3 -> x0, starting transfers between devices: 16.5 us -> none  [the longest x1 5.95 us: per_device(): lax.all_to_all(packed.reshape(worker_groups, greatest_entries, 4, BAND_NO...]
    pallas_call x1, Pallas kernels: 37.2 us -> 49.4 us  [per_device(): pl.pallas_call(window_kernel, out_shape=(jax.ShapeDtypeStruct((NB, OX), j...]
    slice x6 -> x0, local copies, waits for them, and re-layouts: 8.64 us -> none  [the longest x2 3.97 us: padded(): first = lax.slice_in_dim(x, 0, width, axis=dim)]
    ppermute x4 -> x0, starting transfers between devices: 7.34 us -> none  [the longest x2 5.08 us: padded(): after = lax.ppermute(first, axis, down)]
    dot_general x6 -> x0, matrix products: 6.29 us -> none  [the longest x1 2.35 us: per_device(): jnp.einsum('nco,no->nc', coupling_matrix_enlarged, skin_mine, preferred_e...]
    add x2 -> x0, other arithmetic: 4.61 us -> none  [the longest x1 3.94 us: integrate_scalar_once(): heat_deviation + HORIZ_MIX * horizontal_diffusion + VERT_MIX * vertical]
    unnamed x13 -> x3, local copies, waits for them, and re-layouts: 1.5 us -> 4.91 us
    squeeze x2 -> x0, other arithmetic: 2.58 us -> none  [the longest x1 1.54 us: per_device(): marine_interface_transfers[3]]
  transfers between devices with their start and end apart: 7 -> 0, of which waited for: 1 -> 0; matrix products, arithmetic and copies ran while one was open for 25% -> 0% of each run, Pallas kernels for 38% -> 0%
where the time goes in v2:
time: 57.2 us; the launch traced here: 56.9 us
  Pallas kernels  49.4 us (86%)
  local copies, waits for them, and re-layouts  6.28 us (11%)
  between operations  0.65 us (1%)
  other arithmetic  0.63 us (1%)
    pallas_call x1, Pallas kernels, per_device(): pl.pallas_call(window_kernel, out_shape=(jax.ShapeDtypeStruct((NB, OX), j...  49.4 us
    unnamed x3, local copies, waits for them, and re-layouts  4.91 us
    reshape x1, local copies, waits for them, and re-layouts, per_device(): piece_keeper_part.reshape(NB, 1)  1.37 us

profile of v2, /device:TPU:0, one launch (start us, length us, event | category | flops | bytes accessed | tf_op | source)
XLA Modules:
  0.0 56.9 jit_solution(4511652024555504897)
XLA Ops:
  0.6 0.6 %fusion.6.turning = f32[2,128]{1,0:T(2,128)} fusion(s32[1,128]{1,0:T(1,128)S(1)} %get-tuple-element.3, s32[1,128]{1,0:T(1,128)S(1)} %get-tuple-element.4), kind=kLoop, calls=%fused_computation.10 | loop fusion | flops 4608 | bytes 2048 | tf_op jit(solution)/shard_map/mul | solution.py:457
  1.3 1.4 %copy.12.keeper = s32[96,1]{1,0:T(8,128)} copy(s32[96,1]{0,1:T(1,128)} %bitcast.1) | data formatting | bytes 768 | tf_op jit(solution)/shard_map/reshape | solution.py:517
  2.6 49.4 %window.1 = (f32[96,128]{1,0:T(8,128)}, f32[8,128,128]{2,1,0:T(8,128)}, f32[3,128,128]{2,1,0:T(8,128)}) custom-call(bf16[4,96,128]{2,1,0:T(8,128)(2,1)} %sky.1, bf16[96,128,128]{2,1,0:T(8,128)(2,1)} %weights_far.1, s32[96,1]{1,0:T(8,128)} %copy.12.keeper, s32[1,96]{1,0:T(1,128)} %lines.1, s32[128,128]{1,0:T(8,128)} %sea.1, f32[8,128,128]{2,1,0:T(8,128)} %heat.1, ...), custom_call_target="tpu_custom_call" | custom-call | tf_op jit(solution)/shard_map/window/pallas_call | solution.py:482
  52.0 1.4 %copy.16 = f32[96,128]{1,0:T(8,128)} copy(f32[96,128]{1,0:T(8,128)} %get-tuple-element.8) | data formatting | bytes 98304
  53.5 1.9 %copy.17 = f32[8,128,128]{2,1,0:T(8,128)} copy(f32[8,128,128]{2,1,0:T(8,128)} %get-tuple-element.9) | data formatting | bytes 1048576
  55.3 1.6 %copy.18 = f32[3,128,128]{2,1,0:T(8,128)} copy(f32[3,128,128]{2,1,0:T(8,128)} %get-tuple-element.10) | data formatting | bytes 393216
  (1 shorter events, 0.0 us)

commit v3 on v2

--- a/solution.py
+++ b/solution.py
@@ -30,6 +30,7 @@
 SPAN = SUB // 2
 CHUNK = 16
 SLOTS = 8
+FLUXES = 5
 
 
 def low_lanes(rows):
@@ -112,8 +113,8 @@
 
 def place_blocks(keeper, lines, count):
     i, j = line_numbers((NB, NB), 0), line_numbers((NB, NB), 1)
-    owner_col = keeper[...].astype(jnp.float32)
-    owner_row = jnp.sum(jnp.where(i == j, owner_col, 0.0), axis=0, keepdims=True)
+    owner_row = keeper[...].astype(jnp.float32)
+    owner_col = jnp.sum(jnp.where(i == j, owner_row, 0.0), axis=1, keepdims=True)
     same = jnp.where(owner_col == owner_row, 1.0, 0.0)
     rank_row = jnp.sum(jnp.where(i < j, same, 0.0), axis=0, keepdims=True)
     rank_col = jnp.sum(jnp.where(j < i, same, 0.0), axis=1, keepdims=True)
@@ -130,14 +131,20 @@
     place = line_numbers((count * SLOTS, NB), 0)
     slots = as_bits(place == key_row)
     out = []
-    for f in range(4):
-        value = dot(slots, partial[f].astype(jnp.bfloat16))
+    heat_flux = partial[2]
+    heat_high = heat_flux.astype(jnp.bfloat16)
+    heat_low = (heat_flux - heat_high.astype(jnp.float32)).astype(jnp.bfloat16)
+    sources = [partial[f].astype(jnp.bfloat16) for f in range(4)]
+    sources = sources[:2] + [heat_high, sources[3], heat_low]
+    for f in range(FLUXES):
+        value = dot(slots, sources[f])
         if f * spare < most:
             here = (rank_row >= f * spare) & (rank_row < (f + 1) * spare)
             spot = jnp.where(here, key_row - f * spare + most, -1.0)
             value = value + dot(as_bits(place == spot), hot)
         out.append(value.reshape(count, SLOTS, BAND_NORTH_COUNT))
-    for p in range(2):
+    out.append(jnp.zeros_like(out[0]))
+    for p in range(3):
         both = jnp.concatenate([out[2 * p], out[2 * p + 1]], axis=1)
         send[:, 2 * SLOTS * p : 2 * SLOTS * (p + 1), :] = both.astype(jnp.bfloat16)
 
@@ -146,14 +153,14 @@
     spare = SLOTS - most
     total = count * SLOTS
     values = []
-    for p in range(2):
+    for p in range(3):
         both = recv[:, 2 * SLOTS * p : 2 * SLOTS * (p + 1), :].astype(jnp.float32)
         values.append(both[:, :SLOTS].reshape(total, BAND_NORTH_COUNT))
         values.append(both[:, SLOTS:].reshape(total, BAND_NORTH_COUNT))
     slot = lax.broadcasted_iota(jnp.int32, (count, SLOTS, BAND_NORTH_COUNT), 1)
     slot = slot.reshape(total, BAND_NORTH_COUNT)
     target = jnp.zeros((total, BAND_NORTH_COUNT), jnp.float32)
-    for f in range(4):
+    for f in range(FLUXES):
         if f * spare < most:
             moved = pltpu.roll(values[f], total - (most - f * spare), 0)
             here = (slot >= f * spare) & (slot < min((f + 1) * spare, most))
@@ -349,9 +356,9 @@
 
 
 def window_kernel(
-    sky, weights_far, keeper, lines, sea, heat, h_in, u_in, v_in, turning,
+    sky, weights_far, keeper, lines, sea, heat, h_in, u_in, v_in,
     back, heat_out, out,
-    weights, sky32, partial, send, recv, skin_send, skin_recv,
+    turning, weights, sky32, partial, send, recv, skin_send, skin_recv,
     heat_edges, heat_got, tall, near,
     wide, quads1, edge1, side1, quads2, edge2, side2, quads3, edge3, side3,
     load_sem, a2a_send, a2a_recv, skin_send_sem, skin_recv_sem,
@@ -363,6 +370,7 @@
     me = lax.axis_index("gx") * ny + lax.axis_index("gy")
     own = slice(HALF, HALF + OX)
     greet_all(me, count)
+    turning[...] = turning_rows()
     load = pltpu.make_async_copy(weights_far, weights, load_sem)
     load.start()
     lat = lax.axis_index("gy") * BAND_NORTH_COUNT + lax.broadcasted_iota(
@@ -411,7 +419,8 @@
     copies2 = margin_copies(quads2, edge2, side2, send2, recv2)
     for copy in copies2:
         copy.start()
-    surface = heat_out[0] + HEAT_GAIN * dot(target_turned, values[2]) * wide[3, 0, own]
+    heat_flux = dot(target_turned, values[2]) + dot(target_turned, values[4])
+    surface = heat_out[0] + HEAT_GAIN * heat_flux * wide[3, 0, own]
     heat_out[0] = surface
     band = dot(target, surface.astype(jnp.bfloat16))
     skin_send[...] = band.reshape(count, SLOTS, BAND_NORTH_COUNT)
@@ -450,11 +459,31 @@
 
 def turning_rows():
     total_y = lax.axis_size("gy") * BAND_NORTH_COUNT
-    lane = jnp.arange(BAND_NORTH_COUNT, dtype=jnp.int32)
-    own = lax.axis_index("gy") * BAND_NORTH_COUNT + lane
-    far = jnp.where(lane < HALF, own + BAND_NORTH_COUNT, own - BAND_NORTH_COUNT)
-    rows = jnp.mod(jnp.stack([own, far]), total_y)
+    shape = (8, BAND_NORTH_COUNT)
+    lane = lax.broadcasted_iota(jnp.int32, shape, 1)
+    tile = lax.broadcasted_iota(jnp.int32, shape, 0)
+    away = jnp.where(lane < HALF, BAND_NORTH_COUNT, -BAND_NORTH_COUNT)
+    rows = lax.axis_index("gy") * BAND_NORTH_COUNT + lane + jnp.where(tile == 0, 0, away)
+    rows = jnp.where(rows < 0, rows + total_y, jnp.where(rows < total_y, rows, rows - total_y))
     return CORIOLIS * jnp.sin(jnp.pi * ((rows.astype(jnp.float32) + 0.5) / total_y - 0.5))
+
+
+def hand_over(*refs):
+    sources, targets = refs[:3], refs[3:6]
+    buffers, loads, stores = refs[6:9], refs[9], refs[10]
+    into = [
+        pltpu.make_async_copy(sources[k], buffers[k], loads.at[k]) for k in range(3)
+    ]
+    away = [
+        pltpu.make_async_copy(buffers[k], targets[k], stores.at[k]) for k in range(3)
+    ]
+    for copy in into:
+        copy.start()
+    for k in range(3):
+        into[k].wait()
+        away[k].start()
+    for copy in away:
+        copy.wait()
 
 
 def per_device(
@@ -479,21 +508,23 @@
         ]
 
     inside = pl.BlockSpec(memory_space=pltpu.VMEM)
-    return pl.pallas_call(
-        window_kernel,
-        out_shape=(
+    shapes = (
             jax.ShapeDtypeStruct((NB, OX), jnp.float32),
             jax.ShapeDtypeStruct((MARINE_STRATA, OX, line), jnp.float32),
             jax.ShapeDtypeStruct((3, OX, line), jnp.float32),
-        ),
-        in_specs=[inside, pl.BlockSpec(memory_space=pl.ANY)] + [inside] * 8,
+        )
+    results = pl.pallas_call(
+        window_kernel,
+        out_shape=shapes,
+        in_specs=[inside, pl.BlockSpec(memory_space=pl.ANY)] + [inside] * 7,
         out_specs=(inside,) * 3,
         scratch_shapes=[
+            pltpu.VMEM((8, line), jnp.float32),
             pltpu.VMEM((NB, OX, line), jnp.bfloat16),
             pltpu.VMEM((4, NB, OX), jnp.float32),
             pltpu.VMEM((4, NB, line), jnp.float32),
-            pltpu.VMEM((count, 4 * SLOTS, line), jnp.bfloat16),
-            pltpu.VMEM((count, 4 * SLOTS, line), jnp.bfloat16),
+            pltpu.VMEM((count, 6 * SLOTS, line), jnp.bfloat16),
+            pltpu.VMEM((count, 6 * SLOTS, line), jnp.bfloat16),
             pltpu.VMEM((count, SLOTS, line), jnp.float32),
             pltpu.VMEM((count, SLOTS, line), jnp.float32),
             pltpu.VMEM((4, MARINE_STRATA, line), jnp.float32),
@@ -514,15 +545,24 @@
     )(
         sky_interface_transfers,
         coupling_matrix_enlarged,
-        piece_keeper_part.reshape(NB, 1),
+        piece_keeper_part.reshape(1, NB),
         receiving_part_line,
         marine_point_switch,
         potential_heat_deviation,
         free_marine_lift,
         depth_averaged_uflow,
         depth_averaged_vflow,
-        turning_rows(),
-    )
+    )
+    anywhere = pl.BlockSpec(memory_space=pl.ANY)
+    return pl.pallas_call(
+        hand_over,
+        out_shape=shapes,
+        in_specs=[anywhere] * 3,
+        out_specs=(anywhere,) * 3,
+        scratch_shapes=[pltpu.VMEM(shape.shape, jnp.float32) for shape in shapes]
+        + [pltpu.SemaphoreType.DMA((3,))] * 2,
+        name="hand_over",
+    )(*results)
 
 
 def solution(mesh):

time: 57.2 us -> 54.7 us (0.956)
  local copies, waits for them, and re-layouts: 6.28 us -> 0 us
  Pallas kernels: 49.4 us -> 53.9 us
  other arithmetic: 0.63 us -> 0 us
    unnamed x3 -> x0, local copies, waits for them, and re-layouts: 4.91 us -> none
    pallas_call x1 -> x2, Pallas kernels: 49.4 us -> 53.9 us  [the longest x1 51.9 us: per_device(): pl.pallas_call(window_kernel, out_shape=shapes, in_specs=[inside, pl.Bloc...]
    reshape x1 -> x0, local copies, waits for them, and re-layouts: 1.37 us -> none  [per_device(): piece_keeper_part.reshape(NB, 1)]
    mul x1 -> x0, other arithmetic: 0.63 us -> none  [turning_rows(): CORIOLIS * jnp.sin(jnp.pi * ((rows.astype(jnp.float32) + 0.5) / total_y -...]
where the time goes in v3:
time: 54.7 us; the launch traced here: 54.5 us
  Pallas kernels  53.9 us (99%)
  between operations  0.64 us (1%)
    pallas_call x1, Pallas kernels, per_device(): pl.pallas_call(window_kernel, out_shape=shapes, in_specs=[inside, pl.Bloc...  51.9 us
    pallas_call x1, Pallas kernels, per_device(): pl.pallas_call(hand_over, out_shape=shapes, in_specs=[anywhere] * 3, out_...  1.97 us

profile of v3, /device:TPU:0, one launch (start us, length us, event | category | flops | bytes accessed | tf_op | source)
XLA Modules:
  0.0 54.5 jit_solution(5592110031376752918)
XLA Ops:
  0.6 51.9 %window.1 = (f32[96,128]{1,0:T(8,128)}, f32[8,128,128]{2,1,0:T(8,128)}, f32[3,128,128]{2,1,0:T(8,128)}) custom-call(bf16[4,96,128]{2,1,0:T(8,128)(2,1)} %sky.1, bf16[96,128,128]{2,1,0:T(8,128)(2,1)} %weights_far.1, s32[1,96]{1,0:T(1,128)} %bitcast.1, s32[1,96]{1,0:T(1,128)} %lines.1, s32[128,128]{1,0:T(8,128)} %sea.1, f32[8,128,128]{2,1,0:T(8,128)} %heat.1, ...), custom_call_target="tpu_custom_call" | custom-call | tf_op jit(solution)/shard_map/window/pallas_call | solution.py:516
  52.6 2.0 %hand_over.1 = (f32[96,128]{1,0:T(8,128)}, f32[8,128,128]{2,1,0:T(8,128)}, f32[3,128,128]{2,1,0:T(8,128)}) custom-call(f32[96,128]{1,0:T(8,128)} %get-tuple-element.6.refs_0_, f32[8,128,128]{2,1,0:T(8,128)} %get-tuple-element.7.refs_1_, f32[3,128,128]{2,1,0:T(8,128)} %get-tuple-element.8.refs_2_), custom_call_target="tpu_custom_call" | custom-call | tf_op jit(solution)/shard_map/hand_over/pallas_call | solution.py:557
